TPU v7x, 32 devices: a whole 2x2x4 slice. The times are simulated.
32 devices in a mesh: seq: 8 (over z, y), tensor: 4 (over x, core).
Axes of the slice: x: 2, y: 2, z: 4, core: 2. Of those that a mesh axis runs over, the one named last changes fastest.
Arguments:
- fixed_point: bfloat16 [1024, 4096], P(('seq', 'tensor')), may hold values from -6 to 6
- incoming: bfloat16 [1024, 4096], P(('seq', 'tensor')), may hold values from -6 to 6
- norm_gain: float32 [4096], replicated, may hold values from 0.1 to 1.9
- query_weight: bfloat16 [4096, 4096], P(None, 'tensor'), may hold values from -0.21875 to 0.21875, as said below
- key_weight: bfloat16 [4096, 4096], P(None, 'tensor'), may hold values from -0.265625 to 0.265625, as said below
- value_weight: bfloat16 [4096, 4096], P(None, 'tensor'), may hold values from -0.09375 to 0.09375
- out_weight: bfloat16 [4096, 4096], P('tensor'), may hold values from -0.09375 to 0.09375
- layout: int32 [16, 16], replicated, may hold values 0 or 1
Outputs:
- adjoint: float32 [1024, 4096], P(('seq', 'tensor'))
- gain_grad: float32 [4096], replicated
Inputs may be any that keep to these rules, and one draw needn't show every extreme that they name: `query_weight`: entries of the columns of each head are independent; their spread may differ between heads. `key_weight`: entries are independent within a draw; columns of some heads may follow the same head's columns of query_weight. `layout`: A key block strictly before a query block is attended where the entry at row query block, column key block is 1; a block always attends itself causally; entries on or above the diagonal are not read.
All inputs are finite; a program needn't handle non-finite values.
Results may differ from a plain program's by a relative error of at most 0.03.
Values may be sent and summed in bfloat16 or wider, within the bound.
A program may use at most 128 MiB of HBM per device.

v0:
```python
import jax
import jax.numpy as jnp
from jax import lax
from jax.experimental import pallas as pl
from jax.experimental.pallas import tpu as pltpu
from jax.sharding import PartitionSpec as P

HEAD_DIM = 128
BLK = 64
ITERS = 2


EPS = 1e-05
THETA = 10000.0
MASKED = -1e30


def rope_tables(positions):
    freq = THETA ** (-jnp.arange(0, HEAD_DIM, 2, dtype=jnp.float32) / HEAD_DIM)
    angle = positions.astype(jnp.float32)[:, None] * freq[None, :]
    cosine = jnp.concatenate([jnp.cos(angle), jnp.cos(angle)], axis=1)[:, None, :]
    sine = jnp.concatenate([jnp.sin(angle), jnp.sin(angle)], axis=1)[:, None, :]
    return (cosine, sine)


def rotate(values, cosine, sine):
    half = HEAD_DIM // 2
    turned = jnp.concatenate([-values[..., half:], values[..., :half]], axis=-1)
    return values * cosine + turned * sine


def rotate_back(values, cosine, sine):
    half = HEAD_DIM // 2
    weighted = values * sine
    turned = jnp.concatenate([weighted[..., half:], -weighted[..., :half]], axis=-1)
    return values * cosine + turned


def expand_blocks(chosen):
    return jnp.repeat(jnp.repeat(chosen, BLK, axis=0), BLK, axis=1)


def pair_mask(query_pos, key_pos, chosen):
    query_block = (query_pos // BLK)[:, None]
    key_block = (key_pos // BLK)[None, :]
    earlier = (key_block < query_block) & chosen
    same = (key_block == query_block) & (key_pos[None, :] <= query_pos[:, None])
    return earlier | same


def ring_body(
    fixed_point, incoming, norm_gain, query_weight, key_weight, value_weight, out_weight, layout
):
    local_rows, model_width = fixed_point.shape
    head_width = query_weight.shape[1]
    head_count = head_width // HEAD_DIM
    seq_tokens = local_rows * lax.axis_size("tensor")
    seq_length = seq_tokens * lax.axis_size("seq")
    seq_index = lax.axis_index("seq")
    score_scale = HEAD_DIM ** (-0.5)
    contract_last = (((1,), (1,)), ((), ()))
    head_shape = (seq_tokens, head_count, HEAD_DIM)
    point = fixed_point.astype(jnp.float32)
    inv_rms = lax.rsqrt(jnp.mean(point * point, axis=1, keepdims=True) + EPS)
    scaled = point * inv_rms
    normed = (norm_gain * scaled).astype(jnp.bfloat16)
    project_piece = lax.all_gather(normed, "tensor", axis=0, tiled=True)
    projected = jnp.concatenate(
        [
            jnp.dot(project_piece, query_weight, preferred_element_type=jnp.float32),
            jnp.dot(project_piece, key_weight, preferred_element_type=jnp.float32),
            jnp.dot(project_piece, value_weight, preferred_element_type=jnp.float32),
        ],
        axis=1,
    )
    positions = seq_index * seq_tokens + jnp.arange(seq_tokens, dtype=jnp.int32)
    cosine, sine = rope_tables(positions)
    queries = rotate(projected[:, :head_width].reshape(head_shape), cosine, sine).astype(
        jnp.bfloat16
    )
    keys = rotate(
        projected[:, head_width : 2 * head_width].reshape(head_shape), cosine, sine
    ).astype(jnp.bfloat16)
    values = projected[:, 2 * head_width :].reshape(head_shape).astype(jnp.bfloat16)
    block_rows = seq_tokens // BLK
    block_count = seq_length // BLK
    first_block = seq_index * block_rows
    key_positions = jnp.arange(seq_length, dtype=jnp.int32)
    chosen_rows = (
        lax.dynamic_slice(layout, (first_block, jnp.int32(0)), (block_rows, block_count)) > 0
    )
    allowed = pair_mask(positions, key_positions, expand_blocks(chosen_rows))
    keys_all, values_all = (
        lax.all_gather(keys, "seq", axis=0, tiled=True),
        lax.all_gather(values, "seq", axis=0, tiled=True),
    )
    scores = (
        jnp.einsum("qhd,khd->hqk", queries, keys_all, preferred_element_type=jnp.float32)
        * score_scale
    )
    scores = jnp.where(allowed[None], scores, MASKED)
    log_norm = jax.nn.logsumexp(scores, axis=2, keepdims=True)
    probs = jnp.exp(scores - log_norm)
    probs_low = probs.astype(jnp.bfloat16)
    attended = jnp.einsum(
        "hqk,khd->qhd", probs_low, values_all, preferred_element_type=jnp.float32
    ).astype(jnp.bfloat16)
    cotangent = incoming.astype(jnp.float32)
    adjoint = cotangent
    gain_grad = jnp.zeros((model_width,), jnp.float32)
    for term_index in range(ITERS):
        grad_out = lax.dot_general(
            lax.all_gather(cotangent.astype(jnp.bfloat16), "tensor", axis=0, tiled=True),
            out_weight,
            contract_last,
            preferred_element_type=jnp.float32,
        )
        grad_low = grad_out.astype(jnp.bfloat16).reshape(head_shape)
        delta = jnp.sum(grad_low.astype(jnp.float32) * attended.astype(jnp.float32), axis=2)
        grad_probs = jnp.einsum(
            "qhd,khd->hqk", grad_low, values_all, preferred_element_type=jnp.float32
        )
        grad_scores = (probs * (grad_probs - delta.T[:, :, None])).astype(jnp.bfloat16)
        grad_query = (
            jnp.einsum("hqk,khd->qhd", grad_scores, keys_all, preferred_element_type=jnp.float32)
            * score_scale
        )
        key_part = (
            jnp.einsum("hqk,qhd->khd", grad_scores, queries, preferred_element_type=jnp.float32)
            * score_scale
        )
        value_part = jnp.einsum(
            "hqk,qhd->khd", probs_low, grad_low, preferred_element_type=jnp.float32
        )
        key_grads = lax.psum_scatter(
            jnp.concatenate(
                [
                    key_part.reshape(seq_tokens * lax.axis_size("seq"), head_width),
                    value_part.reshape(seq_tokens * lax.axis_size("seq"), head_width),
                ],
                axis=1,
            ).astype(jnp.bfloat16),
            "seq",
            scatter_dimension=0,
            tiled=True,
        ).astype(jnp.float32)
        grad_key = key_grads[:, :head_width].reshape(head_shape)
        grad_value = key_grads[:, head_width:].reshape(head_shape)
        query_low = (
            rotate_back(grad_query, cosine, sine)
            .astype(jnp.bfloat16)
            .reshape(seq_tokens, head_width)
        )
        key_low = (
            rotate_back(grad_key, cosine, sine).astype(jnp.bfloat16).reshape(seq_tokens, head_width)
        )
        value_low = grad_value.astype(jnp.bfloat16).reshape(seq_tokens, head_width)
        total = lax.dot_general(
            query_low, query_weight, contract_last, preferred_element_type=jnp.float32
        )
        total = total + lax.dot_general(
            key_low, key_weight, contract_last, preferred_element_type=jnp.float32
        )
        total = total + lax.dot_general(
            value_low, value_weight, contract_last, preferred_element_type=jnp.float32
        )
        grad_normed = lax.psum_scatter(
            total.astype(jnp.bfloat16), "tensor", scatter_dimension=0, tiled=True
        ).astype(jnp.float32)
        gain_term = jnp.sum(grad_normed * scaled, axis=0)
        gain_grad = gain_grad + lax.psum(gain_term, ("seq", "tensor"))
        weighted = norm_gain * grad_normed
        inner = jnp.sum(weighted * scaled, axis=1, keepdims=True)
        cotangent = inv_rms * (weighted - scaled * (inner / model_width))
        adjoint = adjoint + cotangent
    return (adjoint, gain_grad * seq_length ** (-0.5))


WHOLE, ROWS, COLS = "whole", "rows", "cols"
COMM_BYTES = 80 << 20


def block_view(ref, kind, index, count):
    if kind == WHOLE:
        return ref
    if kind == ROWS:
        size = ref.shape[0] // count
        return ref.at[pl.ds(pl.multiple_of(index * size, size), size), :]
    size = ref.shape[1] // count
    return ref.at[:, pl.ds(pl.multiple_of(index * size, size), size)]


def exchange(arrays, kinds, axis, collective_id):
    count = lax.axis_size(axis)
    number = len(arrays)
    shapes = []
    for array, (source, target) in zip(arrays, kinds):
        rows, cols = array.shape
        rows, cols = {WHOLE: (rows, cols), ROWS: (rows // count, cols), COLS: (rows, cols // count)}[source]
        shape = (rows * count, cols) if target == ROWS else (rows, cols * count)
        shapes.append(jax.ShapeDtypeStruct(shape, array.dtype))

    def kernel(*refs):
        sources, results = refs[:number], refs[number : 2 * number]
        send_sem, recv_sem, own_sem = refs[2 * number :]
        me = lax.axis_index(axis)
        barrier = pltpu.get_barrier_semaphore()
        for step in range(1, count):
            pl.semaphore_signal(
                barrier,
                inc=1,
                device_id={axis: lax.rem(me + step, count)},
                device_id_type=pl.DeviceIdType.MESH,
            )
        pl.semaphore_wait(barrier, count - 1)
        copies = []
        for step in range(1, count):
            peer = lax.rem(me + step, count)
            for item, (source, target) in enumerate(kinds):
                copies.append(
                    pltpu.make_async_remote_copy(
                        src_ref=block_view(sources[item], source, peer, count),
                        dst_ref=block_view(results[item], target, me, count),
                        send_sem=send_sem.at[item, step],
                        recv_sem=recv_sem.at[item, step],
                        device_id={axis: peer},
                        device_id_type=pl.DeviceIdType.MESH,
                    )
                )
                copies[-1].start()
        for item, (source, target) in enumerate(kinds):
            copies.append(
                pltpu.make_async_copy(
                    block_view(sources[item], source, me, count),
                    block_view(results[item], target, me, count),
                    own_sem.at[item],
                )
            )
            copies[-1].start()
        for copy in copies:
            copy.wait()

    moved = sum(shape.size * shape.dtype.itemsize for shape in shapes)
    return pl.pallas_call(
        kernel,
        out_shape=shapes,
        in_specs=[pl.BlockSpec(memory_space=pl.ANY)] * number,
        out_specs=[pl.BlockSpec(memory_space=pl.ANY)] * number,
        scratch_shapes=[
            pltpu.SemaphoreType.DMA((number, count)),
            pltpu.SemaphoreType.DMA((number, count)),
            pltpu.SemaphoreType.DMA((number,)),
        ],
        compiler_params=pltpu.CompilerParams(
            collective_id=collective_id, has_side_effects=True, vmem_limit_bytes=1 << 20
        ),
        cost_estimate=pl.CostEstimate(flops=0, bytes_accessed=COMM_BYTES, transcendentals=0),
    )(*arrays)


def chip_gather(arrays, axis, collective_id):
    count = lax.axis_size(axis)
    number = len(arrays)
    shapes = [jax.ShapeDtypeStruct((a.shape[0] * count, a.shape[1]), a.dtype) for a in arrays]

    def kernel(*refs):
        sources, results = refs[:number], refs[number : 2 * number]
        send_sem, recv_sem, own_sem = refs[2 * number :]
        me = lax.axis_index(axis)
        partner = me + 1 - 2 * lax.rem(me, 2)
        barrier = pltpu.get_barrier_semaphore()
        for peer in [partner] + [lax.rem(me + step, count) for step in range(2, count, 2)]:
            pl.semaphore_signal(
                barrier, inc=1, device_id={axis: peer}, device_id_type=pl.DeviceIdType.MESH
            )
        pl.semaphore_wait(barrier, count // 2)

        def send(item, source, block, peer, slot):
            copy = pltpu.make_async_remote_copy(
                src_ref=source,
                dst_ref=block_view(results[item], ROWS, block, count),
                send_sem=send_sem.at[item, slot],
                recv_sem=recv_sem.at[item, slot],
                device_id={axis: peer},
                device_id_type=pl.DeviceIdType.MESH,
            )
            copy.start()
            return copy

        far, near, own = [], [], []
        for item in range(number):
            for step in range(2, count, 2):
                peer = lax.rem(me + step, count)
                far.append((item, step, send(item, sources[item], me, peer, step)))
        for item in range(number):
            near.append(send(item, sources[item], me, partner, 1))
            own.append(
                pltpu.make_async_copy(
                    sources[item], block_view(results[item], ROWS, me, count), own_sem.at[item]
                )
            )
            own[-1].start()
        for item, step, copy in far:
            copy.wait_recv()
            origin = lax.rem(me - step + count, count)
            block = block_view(results[item], ROWS, origin, count)
            near.append(send(item, block, origin, partner, step + 1))
        for item, step, copy in far:
            copy.wait_send()
        for copy in near + own:
            copy.wait()

    return pl.pallas_call(
        kernel,
        out_shape=shapes,
        in_specs=[pl.BlockSpec(memory_space=pl.ANY)] * number,
        out_specs=[pl.BlockSpec(memory_space=pl.ANY)] * number,
        scratch_shapes=[
            pltpu.SemaphoreType.DMA((number, count)),
            pltpu.SemaphoreType.DMA((number, count)),
            pltpu.SemaphoreType.DMA((number,)),
        ],
        compiler_params=pltpu.CompilerParams(
            collective_id=collective_id, has_side_effects=True, vmem_limit_bytes=1 << 20
        ),
        cost_estimate=pl.CostEstimate(flops=0, bytes_accessed=COMM_BYTES, transcendentals=0),
    )(*arrays)


def chip_scatter(total, axis, collective_id):
    count = lax.axis_size(axis)
    chips = count // 2
    rows, cols = total.shape[0] // count, total.shape[1]
    shape = (chips * rows, cols)

    def kernel(total_ref, result, handed, sums, near_send, near_recv, far_send, far_recv):
        me = lax.axis_index(axis)
        core = lax.rem(me, 2)
        chip = lax.div(me, 2)
        partner = me + 1 - 2 * core
        barrier = pltpu.get_barrier_semaphore()
        for peer in [partner] + [lax.rem(me + step, count) for step in range(2, count, 2)]:
            pl.semaphore_signal(
                barrier, inc=1, device_id={axis: peer}, device_id_type=pl.DeviceIdType.MESH
            )
        pl.semaphore_wait(barrier, chips)
        order = list(range(1, chips)) + [0]
        near, far = [], []
        for step in order:
            target = lax.rem(chip + step, chips)
            copy = pltpu.make_async_remote_copy(
                src_ref=block_view(total_ref, ROWS, 2 * target + 1 - core, count),
                dst_ref=handed.at[pl.ds(step * rows, rows), :],
                send_sem=near_send.at[step],
                recv_sem=near_recv.at[step],
                device_id={axis: partner},
                device_id_type=pl.DeviceIdType.MESH,
            )
            copy.start()
            near.append(copy)
        for step, arrived in zip(order, near):
            arrived.wait_recv()
            target = lax.rem(chip + step, chips)
            place = pl.ds(step * rows, rows)
            own = block_view(total_ref, ROWS, 2 * target + core, count)[...]
            pair = own.astype(jnp.float32) + handed[place, :].astype(jnp.float32)
            if step == 0:
                result[pl.ds(pl.multiple_of(chip * rows, rows), rows), :] = pair.astype(result.dtype)
                continue
            sums[place, :] = pair.astype(sums.dtype)
            copy = pltpu.make_async_remote_copy(
                src_ref=sums.at[place, :],
                dst_ref=block_view(result, ROWS, chip, chips),
                send_sem=far_send.at[step],
                recv_sem=far_recv.at[step],
                device_id={axis: 2 * target + core},
                device_id_type=pl.DeviceIdType.MESH,
            )
            copy.start()
            far.append(copy)
        for copy in near:
            copy.wait_send()
        for copy in far:
            copy.wait()

    return pl.pallas_call(
        kernel,
        out_shape=jax.ShapeDtypeStruct(shape, total.dtype),
        in_specs=[pl.BlockSpec(memory_space=pltpu.VMEM)],
        out_specs=pl.BlockSpec(memory_space=pltpu.VMEM),
        scratch_shapes=[
            pltpu.VMEM(shape, total.dtype),
            pltpu.VMEM(shape, total.dtype),
            pltpu.SemaphoreType.DMA((chips,)),
            pltpu.SemaphoreType.DMA((chips,)),
            pltpu.SemaphoreType.DMA((chips,)),
            pltpu.SemaphoreType.DMA((chips,)),
        ],
        compiler_params=pltpu.CompilerParams(
            collective_id=collective_id, has_side_effects=True, vmem_limit_bytes=8 << 20
        ),
        cost_estimate=pl.CostEstimate(flops=0, bytes_accessed=COMM_BYTES, transcendentals=0),
    )(total)


def sum_blocks(received, count):
    rows = received.shape[0] // count
    total = received[:rows].astype(jnp.float32)
    for index in range(1, count):
        total = total + received[index * rows : (index + 1) * rows].astype(jnp.float32)
    return total


def product(left, right, left_dim, right_dim):
    return lax.dot_general(
        left, right, (((left_dim,), (right_dim,)), ((), ())), preferred_element_type=jnp.float32
    )


def allowed_pairs(layout, length):
    block = jnp.arange(length, dtype=jnp.int32) // BLK
    spread = (block[:, None] == jnp.arange(layout.shape[0], dtype=jnp.int32)[None, :]).astype(
        jnp.bfloat16
    )
    chosen = product(spread, (layout > 0).astype(jnp.bfloat16), 1, 0).astype(jnp.bfloat16)
    chosen = lax.dot_general(
        chosen, spread, (((1,), (1,)), ((), ())), preferred_element_type=jnp.bfloat16
    )
    chosen = chosen > 0.5
    position = jnp.arange(length, dtype=jnp.int32)
    return pair_mask(position, position, chosen)


def head_body(
    fixed_point, incoming, norm_gain, query_weight, key_weight, value_weight, out_weight, layout
):
    local_rows, model_width = fixed_point.shape
    tensor_count = lax.axis_size("tensor")
    seq_count = lax.axis_size("seq")
    head_width = query_weight.shape[1]
    head_count = head_width // HEAD_DIM
    own_heads = head_count // seq_count
    seq_tokens = local_rows * tensor_count
    seq_length = seq_tokens * seq_count
    score_scale = HEAD_DIM ** (-0.5)
    head_shape = (seq_tokens, head_count, HEAD_DIM)
    point = fixed_point.astype(jnp.float32)
    inv_rms = lax.rsqrt(jnp.mean(point * point, axis=1, keepdims=True) + EPS)
    scaled = point * inv_rms
    normed = (norm_gain * scaled).astype(jnp.bfloat16)
    piece, cotangent_piece = chip_gather((normed, incoming), "tensor", 0)
    cosine_all, sine_all = rope_tables(jnp.arange(seq_length, dtype=jnp.int32))
    first = lax.axis_index("seq") * seq_tokens
    cosine = lax.dynamic_slice_in_dim(cosine_all, first, seq_tokens, 0)
    sine = lax.dynamic_slice_in_dim(sine_all, first, seq_tokens, 0)
    cosine_all, sine_all = cosine_all[:, 0], sine_all[:, 0]

    def project(weight):
        return jnp.dot(piece, weight, preferred_element_type=jnp.float32)

    def turned(weight):
        values = rotate(project(weight).reshape(head_shape), cosine, sine)
        return values.astype(jnp.bfloat16).reshape(seq_tokens, head_width)

    grad_first = product(cotangent_piece, out_weight, 1, 1).astype(jnp.bfloat16)
    queries, keys, values, grad_heads = exchange(
        (
            turned(query_weight),
            turned(key_weight),
            project(value_weight).astype(jnp.bfloat16),
            grad_first,
        ),
        ((COLS, ROWS),) * 4,
        "seq",
        1,
    )
    allowed = allowed_pairs(layout, seq_length)
    heads = []
    for head in range(own_heads):
        part = slice(head * HEAD_DIM, (head + 1) * HEAD_DIM)
        query, key, value = queries[:, part], keys[:, part], values[:, part]
        scores = jnp.where(allowed, product(query, key, 1, 1) * score_scale, MASKED)
        probs = jnp.exp(scores - jax.nn.logsumexp(scores, axis=1, keepdims=True))
        probs_low = probs.astype(jnp.bfloat16)
        attended = product(probs_low, value, 1, 0).astype(jnp.bfloat16).astype(jnp.float32)
        heads.append((part, query, key, value, probs, probs_low, attended))
    cotangent = incoming.astype(jnp.float32)
    adjoint = cotangent
    gain_term = jnp.zeros((model_width,), jnp.float32)
    for term_index in range(ITERS):
        base = 2 + 4 * term_index
        if term_index:
            (cotangent_piece,) = chip_gather((cotangent.astype(jnp.bfloat16),), "tensor", base)
            (grad_heads,) = exchange(
                (product(cotangent_piece, out_weight, 1, 1).astype(jnp.bfloat16),),
                ((COLS, ROWS),),
                "seq",
                base + 1,
            )
        grads = []
        for part, query, key, value, probs, probs_low, attended in heads:
            grad_low = grad_heads[:, part]
            delta = jnp.sum(grad_low.astype(jnp.float32) * attended, axis=1, keepdims=True)
            grad_probs = product(grad_low, value, 1, 1)
            grad_scores = (probs * (grad_probs - delta)).astype(jnp.bfloat16)
            grad_query = product(grad_scores, key, 1, 0) * score_scale
            grad_key = product(grad_scores, query, 0, 0) * score_scale
            grad_value = product(probs_low, grad_low, 0, 0)
            grads.append(
                (
                    rotate_back(grad_query, cosine_all, sine_all).astype(jnp.bfloat16),
                    rotate_back(grad_key, cosine_all, sine_all).astype(jnp.bfloat16),
                    grad_value.astype(jnp.bfloat16),
                )
            )
        query_low, key_low, value_low = exchange(
            tuple(jnp.concatenate(items, axis=1) for items in zip(*grads)),
            ((ROWS, COLS),) * 3,
            "seq",
            base + 2,
        )
        total = product(query_low, query_weight, 1, 1)
        total = total + product(key_low, key_weight, 1, 1)
        total = total + product(value_low, value_weight, 1, 1)
        received = chip_scatter(total.astype(jnp.bfloat16), "tensor", base + 3)
        grad_normed = sum_blocks(received, tensor_count // 2)
        gain_term = gain_term + jnp.sum(grad_normed * scaled, axis=0)
        weighted = norm_gain * grad_normed
        inner = jnp.sum(weighted * scaled, axis=1, keepdims=True)
        cotangent = inv_rms * (weighted - scaled * (inner / model_width))
        adjoint = adjoint + cotangent
    shape = (8, model_width // 8)
    for axis, collective_id in (("tensor", 2 + 4 * ITERS), ("seq", 3 + 4 * ITERS)):
        (received,) = exchange((gain_term.reshape(shape),), ((WHOLE, ROWS),), axis, collective_id)
        gain_term = jnp.sum(received.reshape(-1, *shape), axis=0).reshape(-1)
    return (adjoint, gain_term * seq_length ** (-0.5))


def solution(mesh):
    in_specs = (
        P(("seq", "tensor"), None),
        P(("seq", "tensor"), None),
        P(),
        P(None, "tensor"),
        P(None, "tensor"),
        P(None, "tensor"),
        P("tensor", None),
        P(),
    )
    out_specs = (P(("seq", "tensor"), None), P())
    whole_heads = mesh.shape["tensor"] * mesh.shape["seq"]

    def body(*arrays):
        heads = arrays[3].shape[1] * mesh.shape["tensor"] // HEAD_DIM
        even = mesh.shape["tensor"] % 2 == 0
        chosen = head_body if even and heads % whole_heads == 0 else ring_body
        return chosen(*arrays)

    return jax.shard_map(body, mesh=mesh, in_specs=in_specs, out_specs=out_specs, check_vma=False)
```

profile of v0, /device:TPU:0, one launch (start us, length us, event | category | flops | bytes accessed | tf_op | source)
XLA Modules:
  0.0 209.6 jit_solution(5820123638277616854)
XLA Ops:
  2.9 1.9 multiply_cosine_fusion
  6.7 16.9 %shard_map.95 = (bf16[128,4096]{1,0:T(8,128)(2,1)S(1)}, bf16[128,4096]{1,0:T(8,128)(2,1)S(1)}) custom-call(bf16[32,4096]{1,0:T(8,128)(2,1)S(1)} %fusion.14.refs_0_, bf16[32,4096]{1,0:T(8,128)(2,1)S(1)} %copy-done), custom_call_target="tpu_custom_call" | custom-call | bytes 83886080 | tf_op jit(solution)/shard_map/pallas_call | solution.py:313
  23.6 6.5 %convolution_convert_fusion.4.refs_3_ = bf16[128,1024]{1,0:T(8,128)(2,1)S(1)} fusion(bf16[128,4096]{1,0:T(8,128)(2,1)S(1)} %get-tuple-element.15, bf16[1024,4096]{1,0:T(8,128)(2,1)} %param.14), kind=kOutput, calls=%fused_computation.24 | convolution fusion | flops 1073872896 | bytes 9699328 | tf_op jit(solution)/shard_map/dot_general | solution.py:415
  30.2 1.3 convolution_convert_fusion.5.refs_2_
  33.6 1.4 slice-done.1
  35.0 1.3 fusion.56
  37.8 22.6 %shard_map.96 = (bf16[1024,128]{1,0:T(8,128)(2,1)S(1)}, bf16[1024,128]{1,0:T(8,128)(2,1)S(1)}, bf16[1024,128]{1,0:T(8,128)(2,1)S(1)}, bf16[1024,128]{1,0:T(8,128)(2,1)S(1)}) custom-call(bf16[128,1024]{1,0:T(8,128)(2,1)S(1)} %get-tuple-element.47.refs_0_, bf16[128,1024]{1,0:T(8,128)(2,1)S(1)} %get-tuple-element.46.refs_1_, ...), custom_call_target="tpu_custom_call" | custom-call | bytes 83886080 | tf_op jit(solution)/shard_map/pallas_call | solution.py:244
  61.3 1.5 fusion.55
  64.8 1.8 multiply_reduce_fusion.1
  70.2 22.7 %shard_map.97 = (bf16[128,1024]{1,0:T(8,128)(2,1)S(1)}, bf16[128,1024]{1,0:T(8,128)(2,1)S(1)}, bf16[128,1024]{1,0:T(8,128)(2,1)S(1)}) custom-call(bf16[1024,128]{1,0:T(8,128)(2,1)S(1)} %get-tuple-element.39.refs_0_, bf16[1024,128]{1,0:T(8,128)(2,1)S(1)} %get-tuple-element.38.refs_1_, bf16[1024,128]{1,0:T(8,128)(2,1)S(1)} %convolution_convert_fusion.2.refs_2_), custom_call_target="tpu_custom_call" | custom-call | bytes 83886080 | tf_op jit(solution)/shard_map/pallas_call | solution.py:244
  92.9 4.2 %fusion.58 = f32[128,4096]{1,0:T(8,128)} fusion(bf16[128,1024]{1,0:T(8,128)(2,1)S(1)} %get-tuple-element.20, bf16[4096,1024]{1,0:T(8,128)(2,1)S(1)} %bitcast.74), kind=kOutput, calls=%fused_computation.120 | convolution fusion | flops 1073741824 | bytes 10747904 | tf_op jit(solution)/shard_map/dot_general | solution.py:415
  97.1 4.5 %convolution_add_fusion.3 = f32[128,4096]{1,0:T(8,128)S(1)} fusion(f32[128,4096]{1,0:T(8,128)} %fusion.58, bf16[128,1024]{1,0:T(8,128)(2,1)S(1)} %get-tuple-element.21, bf16[4096,1024]{1,0:T(8,128)(2,1)S(1)} %bitcast.78), kind=kOutput, calls=%fused_computation.3 | convolution fusion | flops 1074266112 | bytes 12845056 | tf_op jit(solution)/shard_map/dot_general | solution.py:415
  101.6 6.3 %fusion.total_ref = bf16[128,4096]{1,0:T(8,128)(2,1)S(1)} fusion(f32[128,4096]{1,0:T(8,128)S(1)} %convolution_add_fusion.3, bf16[128,1024]{1,0:T(8,128)(2,1)S(1)} %get-tuple-element.22, bf16[4096,1024]{1,0:T(8,128)(2,1)} %param.13), kind=kOutput, calls=%fused_computation.4 | convolution fusion | flops 1074790400 | bytes 11796480 | tf_op jit(solution)/shard_map/dot_general | solution.py:415
  107.9 9.7 %shard_map.98 = bf16[64,4096]{1,0:T(8,128)(2,1)S(1)} custom-call(bf16[128,4096]{1,0:T(8,128)(2,1)S(1)} %fusion.total_ref), custom_call_target="tpu_custom_call" | custom-call | bytes 83886080 | tf_op jit(solution)/shard_map/pallas_call | solution.py:386
  118.1 9.6 %shard_map.99 = bf16[128,4096]{1,0:T(8,128)(2,1)S(1)} custom-call(bf16[32,4096]{1,0:T(8,128)(2,1)S(1)} %fusion.33.refs_0_), custom_call_target="tpu_custom_call" | custom-call | bytes 83886080 | tf_op jit(solution)/shard_map/pallas_call | solution.py:313
  127.7 6.5 %convolution_convert_fusion.1.refs_0_ = bf16[128,1024]{1,0:T(8,128)(2,1)S(1)} fusion(bf16[128,4096]{1,0:T(8,128)(2,1)S(1)} %shard_map.99, bf16[1024,4096]{1,0:T(8,128)(2,1)} %param.14), kind=kOutput, calls=%fused_computation.20 | convolution fusion | flops 1073872896 | bytes 9699328 | tf_op jit(solution)/shard_map/dot_general | solution.py:415
  134.2 13.8 %shard_map.100 = bf16[1024,128]{1,0:T(8,128)(2,1)S(1)} custom-call(bf16[128,1024]{1,0:T(8,128)(2,1)S(1)} %convolution_convert_fusion.1.refs_0_), custom_call_target="tpu_custom_call" | custom-call | bytes 83886080 | tf_op jit(solution)/shard_map/pallas_call | solution.py:244
  152.3 17.6 %shard_map.101 = (bf16[128,1024]{1,0:T(8,128)(2,1)S(1)}, bf16[128,1024]{1,0:T(8,128)(2,1)S(1)}, bf16[128,1024]{1,0:T(8,128)(2,1)S(1)}) custom-call(bf16[1024,128]{1,0:T(8,128)(2,1)S(1)} %get-tuple-element.31.refs_0_, bf16[1024,128]{1,0:T(8,128)(2,1)S(1)} %get-tuple-element.30.refs_1_, bf16[1024,128]{1,0:T(8,128)(2,1)S(1)} %convolution_convert_fusion.refs_2_), custom_call_target="tpu_custom_call" | custom-call | bytes 83886080 | tf_op jit(solution)/shard_map/pallas_call | solution.py:244
  169.9 2.9 %fusion.59 = f32[128,4096]{1,0:T(8,128)S(1)} fusion(bf16[128,1024]{1,0:T(8,128)(2,1)S(1)} %get-tuple-element.23, bf16[4096,1024]{1,0:T(8,128)(2,1)S(1)} %bitcast.74), kind=kOutput, calls=%fused_computation.121 | convolution fusion | flops 1073741824 | bytes 10747904 | tf_op jit(solution)/shard_map/dot_general | solution.py:415
  172.8 2.9 %convolution_add_fusion.1 = f32[128,4096]{1,0:T(8,128)S(1)} fusion(f32[128,4096]{1,0:T(8,128)S(1)} %fusion.59, bf16[128,1024]{1,0:T(8,128)(2,1)S(1)} %get-tuple-element.24, bf16[4096,1024]{1,0:T(8,128)(2,1)S(1)} %bitcast.78), kind=kOutput, calls=%fused_computation.1 | convolution fusion | flops 1074266112 | bytes 12845056 | tf_op jit(solution)/shard_map/dot_general | solution.py:415
  175.8 6.3 %fusion.1.total_ref = bf16[128,4096]{1,0:T(8,128)(2,1)S(1)} fusion(f32[128,4096]{1,0:T(8,128)S(1)} %convolution_add_fusion.1, bf16[128,1024]{1,0:T(8,128)(2,1)S(1)} %get-tuple-element.25, bf16[4096,1024]{1,0:T(8,128)(2,1)} %param.13), kind=kOutput, calls=%fused_computation.5 | convolution fusion | flops 1074790400 | bytes 11796480 | tf_op jit(solution)/shard_map/dot_general | solution.py:415
  182.1 9.3 %shard_map.102 = bf16[64,4096]{1,0:T(8,128)(2,1)S(1)} custom-call(bf16[128,4096]{1,0:T(8,128)(2,1)S(1)} %fusion.1.total_ref), custom_call_target="tpu_custom_call" | custom-call | bytes 83886080 | tf_op jit(solution)/shard_map/pallas_call | solution.py:386
  192.9 3.8 %shard_map.103 = f32[32,512]{1,0:T(8,128)S(1)} custom-call(f32[8,512]{1,0:T(8,128)S(1)} %add.102.refs_0_), custom_call_target="tpu_custom_call" | custom-call | bytes 83886080 | tf_op jit(solution)/shard_map/pallas_call | solution.py:244
  196.7 11.8 %shard_map.104 = f32[64,512]{1,0:T(8,128)S(1)} custom-call(f32[8,512]{1,0:T(8,128)S(1)} %bitcast_reduce_fusion.1.refs_0_), custom_call_target="tpu_custom_call" | custom-call | bytes 83886080 | tf_op jit(solution)/shard_map/pallas_call | solution.py:244
  (97 shorter events, 20.9 us)
Async XLA Ops:
  4.8 0.8 copy-start.7
  4.8 1.0 copy-start.10
  5.8 1.0 copy-start
  6.7 23.4 %copy-start.2 = (bf16[4096,1024]{1,0:T(8,128)(2,1)S(1)}, bf16[4096,1024]{1,0:T(8,128)(2,1)}, u32[]{:S(2)}) copy-start(bf16[4096,1024]{1,0:T(8,128)(2,1)} %param.13) | copy-start | bytes 25165828
  23.6 7.8 %slice-start.4 = ((s8[8388608]{0:T(1024)(128)(4,1)}), s8[4194304]{0:T(1024)(128)(4,1)S(1)}, s32[]{:S(2)}) async-start(s8[8388608]{0:T(1024)(128)(4,1)} %bitcast.75), calls=%async_computation.4 | async-start | bytes 8388608
  30.1 2.2 %slice-start.5 = ((s8[8388608]{0:T(1024)(128)(4,1)}), s8[4194304]{0:T(1024)(128)(4,1)S(1)}, s32[]{:S(2)}) async-start(s8[8388608]{0:T(1024)(128)(4,1)} %bitcast.75), calls=%async_computation.5 | async-start | bytes 8388608
  30.1 3.5 %slice-start = ((s8[8388608]{0:T(1024)(128)(4,1)}), s8[4194304]{0:T(1024)(128)(4,1)S(1)}, s32[]{:S(2)}) async-start(s8[8388608]{0:T(1024)(128)(4,1)} %bitcast.71), calls=%async_computation | async-start | bytes 8388608
  32.3 2.7 %slice-start.1 = ((s8[8388608]{0:T(1024)(128)(4,1)}), s8[4194304]{0:T(1024)(128)(4,1)S(1)}, s32[]{:S(2)}) async-start(s8[8388608]{0:T(1024)(128)(4,1)} %bitcast.71), calls=%async_computation.1 | async-start | bytes 8388608
  36.9 23.4 %copy-start.15 = (s32[16,16]{1,0:T(8,128)S(1)}, s32[16,16]{1,0:T(8,128)}, u32[]{:S(2)}) copy-start(s32[16,16]{1,0:T(8,128)} %param.15) | copy-start | bytes 3076
  62.8 3.8 %copy-start.3 = (f32[1024,1024]{0,1:T(8,128)}, f32[1024,1024]{0,1:T(8,128)S(1)}, u32[]{:S(2)}) copy-start(f32[1024,1024]{0,1:T(8,128)S(1)} %get-tuple-element.57) | copy-start | bytes 12582916
  66.6 1.6 copy-start.8
  67.5 25.4 %slice-start.2 = ((s8[8388608]{0:T(1024)(128)(4,1)}), s8[4194304]{0:T(1024)(128)(4,1)S(1)}, s32[]{:S(2)}) async-start(s8[8388608]{0:T(1024)(128)(4,1)} %bitcast.73), calls=%async_computation.2 | async-start | bytes 8388608
  68.2 1.4 copy-start.11
  68.3 24.6 %slice-start.3 = ((s8[8388608]{0:T(1024)(128)(4,1)}), s8[4194304]{0:T(1024)(128)(4,1)S(1)}, s32[]{:S(2)}) async-start(s8[8388608]{0:T(1024)(128)(4,1)} %bitcast.73), calls=%async_computation.3 | async-start | bytes 8388608
  69.7 27.5 %slice-start.6 = ((s8[8388608]{0:T(1024)(128)(4,1)}), s8[4194304]{0:T(1024)(128)(4,1)S(1)}, s32[]{:S(2)}) async-start(s8[8388608]{0:T(1024)(128)(4,1)} %bitcast.77), calls=%async_computation.6 | async-start | bytes 8388608
  92.9 4.3 %slice-start.7 = ((s8[8388608]{0:T(1024)(128)(4,1)}), s8[4194304]{0:T(1024)(128)(4,1)S(1)}, s32[]{:S(2)}) async-start(s8[8388608]{0:T(1024)(128)(4,1)} %bitcast.77), calls=%async_computation.7 | async-start | bytes 8388608
  101.6 16.0 %copy-start.5 = (bf16[32,4096]{1,0:T(8,128)(2,1)S(1)}, bf16[32,4096]{1,0:T(8,128)(2,1)}, u32[]{:S(2)}) copy-start(bf16[32,4096]{1,0:T(8,128)(2,1)} %param.8) | copy-start | bytes 786436
  101.6 16.0 %copy-start.14 = (f32[4096]{0:T(1024)S(1)}, f32[4096]{0:T(1024)}, u32[]{:S(2)}) copy-start(f32[4096]{0:T(1024)} %param.10) | copy-start | bytes 49156
  127.7 21.1 %copy-start.13 = (f32[1024,128]{1,0:T(8,128)S(1)}, f32[1024,128]{1,0:T(8,128)}, u32[]{:S(2)}) copy-start(f32[1024,128]{1,0:T(8,128)} %get-tuple-element.59) | copy-start | bytes 1572868
  127.7 21.3 %copy-start.4 = (f32[1024,1024]{0,1:T(8,128)S(1)}, f32[1024,1024]{0,1:T(8,128)}, u32[]{:S(2)}) copy-start(f32[1024,1024]{0,1:T(8,128)} %copy-done.3) | copy-start | bytes 12582916
  149.0 1.7 copy-start.9
  150.7 1.1 copy-start.12
  175.7 16.0 %copy-start.1 = (bf16[32,4096]{1,0:T(8,128)(2,1)S(1)}, bf16[32,4096]{1,0:T(8,128)(2,1)}, u32[]{:S(2)}) copy-start(bf16[32,4096]{1,0:T(8,128)(2,1)} %refs_1_.1) | copy-start | bytes 786436
  175.7 16.0 %copy-start.6 = (bf16[32,4096]{1,0:T(8,128)(2,1)S(1)}, bf16[32,4096]{1,0:T(8,128)(2,1)}, u32[]{:S(2)}) copy-start(bf16[32,4096]{1,0:T(8,128)(2,1)} %param.8) | copy-start | bytes 786436
where the time goes:
time: 212 us; the launch traced here: 210 us
  Pallas kernels  138 us (65%)
  matrix products  54.2 us (26%)
  other arithmetic  10.6 us (5%)
  local copies, waits for them, and re-layouts  5.32 us (3%)
    pallas_call x6, Pallas kernels, exchange(): pl.pallas_call(kernel, out_shape=shapes, in_specs=[pl.BlockSpec(memory_sp...  92.3 us
    dot_general x18, matrix products, product(): lax.dot_general(left, right, (((left_dim,), (right_dim,)), ((), ())), pre...  49.4 us
    pallas_call x2, Pallas kernels, chip_gather(): pl.pallas_call(kernel, out_shape=shapes, in_specs=[pl.BlockSpec(memory_sp...  26.5 us
    pallas_call x2, Pallas kernels, chip_scatter(): pl.pallas_call(kernel, out_shape=jax.ShapeDtypeStruct(shape, total.dtype)...  19 us
    unnamed x51, local copies, waits for them, and re-layouts  5.28 us

commit v1 on v0

v1 whole, which is shorter than its diff:
```python
import types

import jax
import jax.numpy as jnp
import numpy as np
from jax import lax
from jax.experimental import pallas as pl
from jax.experimental.pallas import tpu as pltpu
from jax.sharding import PartitionSpec as P

HEAD_DIM = 128
BLK = 64
ITERS = 2


EPS = 1e-05
THETA = 10000.0
MASKED = -1e30


def rope_tables(positions):
    freq = THETA ** (-jnp.arange(0, HEAD_DIM, 2, dtype=jnp.float32) / HEAD_DIM)
    angle = positions.astype(jnp.float32)[:, None] * freq[None, :]
    cosine = jnp.concatenate([jnp.cos(angle), jnp.cos(angle)], axis=1)[:, None, :]
    sine = jnp.concatenate([jnp.sin(angle), jnp.sin(angle)], axis=1)[:, None, :]
    return (cosine, sine)


def rotate(values, cosine, sine):
    half = HEAD_DIM // 2
    turned = jnp.concatenate([-values[..., half:], values[..., :half]], axis=-1)
    return values * cosine + turned * sine


def rotate_back(values, cosine, sine):
    half = HEAD_DIM // 2
    weighted = values * sine
    turned = jnp.concatenate([weighted[..., half:], -weighted[..., :half]], axis=-1)
    return values * cosine + turned


def expand_blocks(chosen):
    return jnp.repeat(jnp.repeat(chosen, BLK, axis=0), BLK, axis=1)


def pair_mask(query_pos, key_pos, chosen):
    query_block = (query_pos // BLK)[:, None]
    key_block = (key_pos // BLK)[None, :]
    earlier = (key_block < query_block) & chosen
    same = (key_block == query_block) & (key_pos[None, :] <= query_pos[:, None])
    return earlier | same


def ring_body(
    fixed_point, incoming, norm_gain, query_weight, key_weight, value_weight, out_weight, layout
):
    local_rows, model_width = fixed_point.shape
    head_width = query_weight.shape[1]
    head_count = head_width // HEAD_DIM
    seq_tokens = local_rows * lax.axis_size("tensor")
    seq_length = seq_tokens * lax.axis_size("seq")
    seq_index = lax.axis_index("seq")
    score_scale = HEAD_DIM ** (-0.5)
    contract_last = (((1,), (1,)), ((), ()))
    head_shape = (seq_tokens, head_count, HEAD_DIM)
    point = fixed_point.astype(jnp.float32)
    inv_rms = lax.rsqrt(jnp.mean(point * point, axis=1, keepdims=True) + EPS)
    scaled = point * inv_rms
    normed = (norm_gain * scaled).astype(jnp.bfloat16)
    project_piece = lax.all_gather(normed, "tensor", axis=0, tiled=True)
    projected = jnp.concatenate(
        [
            jnp.dot(project_piece, query_weight, preferred_element_type=jnp.float32),
            jnp.dot(project_piece, key_weight, preferred_element_type=jnp.float32),
            jnp.dot(project_piece, value_weight, preferred_element_type=jnp.float32),
        ],
        axis=1,
    )
    positions = seq_index * seq_tokens + jnp.arange(seq_tokens, dtype=jnp.int32)
    cosine, sine = rope_tables(positions)
    queries = rotate(projected[:, :head_width].reshape(head_shape), cosine, sine).astype(
        jnp.bfloat16
    )
    keys = rotate(
        projected[:, head_width : 2 * head_width].reshape(head_shape), cosine, sine
    ).astype(jnp.bfloat16)
    values = projected[:, 2 * head_width :].reshape(head_shape).astype(jnp.bfloat16)
    block_rows = seq_tokens // BLK
    block_count = seq_length // BLK
    first_block = seq_index * block_rows
    key_positions = jnp.arange(seq_length, dtype=jnp.int32)
    chosen_rows = (
        lax.dynamic_slice(layout, (first_block, jnp.int32(0)), (block_rows, block_count)) > 0
    )
    allowed = pair_mask(positions, key_positions, expand_blocks(chosen_rows))
    keys_all, values_all = (
        lax.all_gather(keys, "seq", axis=0, tiled=True),
        lax.all_gather(values, "seq", axis=0, tiled=True),
    )
    scores = (
        jnp.einsum("qhd,khd->hqk", queries, keys_all, preferred_element_type=jnp.float32)
        * score_scale
    )
    scores = jnp.where(allowed[None], scores, MASKED)
    log_norm = jax.nn.logsumexp(scores, axis=2, keepdims=True)
    probs = jnp.exp(scores - log_norm)
    probs_low = probs.astype(jnp.bfloat16)
    attended = jnp.einsum(
        "hqk,khd->qhd", probs_low, values_all, preferred_element_type=jnp.float32
    ).astype(jnp.bfloat16)
    cotangent = incoming.astype(jnp.float32)
    adjoint = cotangent
    gain_grad = jnp.zeros((model_width,), jnp.float32)
    for term_index in range(ITERS):
        grad_out = lax.dot_general(
            lax.all_gather(cotangent.astype(jnp.bfloat16), "tensor", axis=0, tiled=True),
            out_weight,
            contract_last,
            preferred_element_type=jnp.float32,
        )
        grad_low = grad_out.astype(jnp.bfloat16).reshape(head_shape)
        delta = jnp.sum(grad_low.astype(jnp.float32) * attended.astype(jnp.float32), axis=2)
        grad_probs = jnp.einsum(
            "qhd,khd->hqk", grad_low, values_all, preferred_element_type=jnp.float32
        )
        grad_scores = (probs * (grad_probs - delta.T[:, :, None])).astype(jnp.bfloat16)
        grad_query = (
            jnp.einsum("hqk,khd->qhd", grad_scores, keys_all, preferred_element_type=jnp.float32)
            * score_scale
        )
        key_part = (
            jnp.einsum("hqk,qhd->khd", grad_scores, queries, preferred_element_type=jnp.float32)
            * score_scale
        )
        value_part = jnp.einsum(
            "hqk,qhd->khd", probs_low, grad_low, preferred_element_type=jnp.float32
        )
        key_grads = lax.psum_scatter(
            jnp.concatenate(
                [
                    key_part.reshape(seq_tokens * lax.axis_size("seq"), head_width),
                    value_part.reshape(seq_tokens * lax.axis_size("seq"), head_width),
                ],
                axis=1,
            ).astype(jnp.bfloat16),
            "seq",
            scatter_dimension=0,
            tiled=True,
        ).astype(jnp.float32)
        grad_key = key_grads[:, :head_width].reshape(head_shape)
        grad_value = key_grads[:, head_width:].reshape(head_shape)
        query_low = (
            rotate_back(grad_query, cosine, sine)
            .astype(jnp.bfloat16)
            .reshape(seq_tokens, head_width)
        )
        key_low = (
            rotate_back(grad_key, cosine, sine).astype(jnp.bfloat16).reshape(seq_tokens, head_width)
        )
        value_low = grad_value.astype(jnp.bfloat16).reshape(seq_tokens, head_width)
        total = lax.dot_general(
            query_low, query_weight, contract_last, preferred_element_type=jnp.float32
        )
        total = total + lax.dot_general(
            key_low, key_weight, contract_last, preferred_element_type=jnp.float32
        )
        total = total + lax.dot_general(
            value_low, value_weight, contract_last, preferred_element_type=jnp.float32
        )
        grad_normed = lax.psum_scatter(
            total.astype(jnp.bfloat16), "tensor", scatter_dimension=0, tiled=True
        ).astype(jnp.float32)
        gain_term = jnp.sum(grad_normed * scaled, axis=0)
        gain_grad = gain_grad + lax.psum(gain_term, ("seq", "tensor"))
        weighted = norm_gain * grad_normed
        inner = jnp.sum(weighted * scaled, axis=1, keepdims=True)
        cotangent = inv_rms * (weighted - scaled * (inner / model_width))
        adjoint = adjoint + cotangent
    return (adjoint, gain_grad * seq_length ** (-0.5))


CHUNKS = 4
MESH = pl.DeviceIdType.MESH


def numpy_tables(length):
    freq = np.float32(THETA) ** (-np.arange(0, HEAD_DIM, 2, dtype=np.float32) / np.float32(HEAD_DIM))
    angle = np.arange(length, dtype=np.float32)[:, None] * freq.astype(np.float32)[None, :]
    cosine = np.cos(angle.astype(np.float64)).astype(np.float32)
    sine = np.sin(angle.astype(np.float64)).astype(np.float32)
    return np.concatenate([cosine, cosine], axis=1), np.concatenate([-sine, sine], axis=1)


def product(left, right, left_dim, right_dim):
    return lax.dot_general(
        left, right, (((left_dim,), (right_dim,)), ((), ())), preferred_element_type=jnp.float32
    )


def flipped(index, mask, bits):
    result = 0
    for bit in range(bits):
        here = lax.rem(lax.div(index, 1 << bit), 2)
        result = result + (1 << bit) * ((1 - here) if (mask >> bit) & 1 else here)
    return result


def window(index, size):
    return pl.ds(pl.multiple_of(index * size, size), size)


def fused_body(
    fixed_point, incoming, norm_gain, query_weight, key_weight, value_weight, out_weight, layout
):
    rows, width = fixed_point.shape
    tensor_count = lax.axis_size("tensor")
    seq_count = lax.axis_size("seq")
    chips = tensor_count // 2
    bits = seq_count.bit_length() - 1
    head_width = query_weight.shape[1]
    tokens = rows * tensor_count
    length = tokens * seq_count
    blocks = layout.shape[0]
    part = width // CHUNKS
    score_scale = HEAD_DIM ** (-0.5)
    gain_rows = width // HEAD_DIM
    gain_part = gain_rows // CHUNKS
    cosine, sine = numpy_tables(length)
    order = list(range(seq_count - 1, 0, -1))
    low, full = jnp.bfloat16, jnp.float32
    dma = pltpu.SemaphoreType.DMA
    hops = 2 * chips - 1
    scratch = {
        "wq": pltpu.VMEM((width, head_width), low),
        "wk": pltpu.VMEM((width, head_width), low),
        "wv": pltpu.VMEM((width, head_width), low),
        "wo": pltpu.VMEM((head_width, width), low),
        "point": pltpu.VMEM((rows, width), low),
        "gain": pltpu.VMEM((1, width), full),
        "layout": pltpu.VMEM(layout.shape, jnp.int32),
        "cosine": pltpu.VMEM((length, HEAD_DIM), full),
        "sine": pltpu.VMEM((length, HEAD_DIM), full),
        "bias": pltpu.VMEM((blocks, length), full),
        "scaled": pltpu.VMEM((rows, width), full),
        "pieces": pltpu.VMEM((1 + ITERS, tokens, width), low),
        "acc": pltpu.VMEM((4, tokens, head_width), full),
        "heads_out": pltpu.VMEM((3 + ITERS, seq_count, tokens, HEAD_DIM), low),
        "heads_in": pltpu.VMEM((3 + ITERS, length, HEAD_DIM), low),
        "probs": pltpu.VMEM((length, length), low),
        "key_acc": pltpu.VMEM((length, HEAD_DIM), full),
        "value_acc": pltpu.VMEM((length, HEAD_DIM), full),
        "grads_out": pltpu.VMEM((3 * ITERS, length, HEAD_DIM), low),
        "grads_in": pltpu.VMEM((3 * ITERS, tokens, head_width), low),
        "total": pltpu.VMEM((tokens, width), full),
        "hand_out": pltpu.VMEM((ITERS * chips, rows, width), low),
        "hand_in": pltpu.VMEM((ITERS * chips, rows, width), low),
        "far_out": pltpu.VMEM((ITERS * chips, rows, width), low),
        "far_in": pltpu.VMEM((ITERS * chips, rows, width), low),
        "normed_grad": pltpu.VMEM((rows, width), full),
        "adjoint": pltpu.VMEM((rows, width), full),
        "gain_sum": pltpu.VMEM((1, width), full),
        "gain_own": pltpu.VMEM((gain_rows, HEAD_DIM), full),
        "gain_near": pltpu.VMEM((tensor_count, gain_rows, HEAD_DIM), full),
        "gain_mid": pltpu.VMEM((gain_rows, HEAD_DIM), full),
        "gain_far": pltpu.VMEM((seq_count, gain_rows, HEAD_DIM), full),
        "gain_out": pltpu.VMEM((gain_rows, HEAD_DIM), full),
        "load_sem": dma((7,)),
        "weight_sem": dma((4, CHUNKS)),
        "gather_send": dma((1 + ITERS, CHUNKS, hops)),
        "gather_recv": dma((1 + ITERS, CHUNKS, hops)),
        "heads_send": dma((3 + ITERS, seq_count)),
        "heads_recv": dma((3 + ITERS, seq_count)),
        "grads_send": dma((3 * ITERS, seq_count)),
        "grads_recv": dma((3 * ITERS, seq_count)),
        "hand_send": dma((ITERS * chips, CHUNKS)),
        "hand_recv": dma((ITERS * chips, CHUNKS)),
        "far_send": dma((ITERS * chips, CHUNKS)),
        "far_recv": dma((ITERS * chips, CHUNKS)),
        "near_send": dma((tensor_count, CHUNKS)),
        "near_recv": dma((tensor_count, CHUNKS)),
        "wide_send": dma((seq_count, CHUNKS)),
        "wide_recv": dma((seq_count, CHUNKS)),
    }

    def kernel(*refs):
        point_hbm, incoming_hbm, gain_hbm, wq_hbm, wk_hbm, wv_hbm, wo_hbm = refs[:7]
        layout_hbm, cosine_hbm, sine_hbm, adjoint_hbm, gain_out_hbm = refs[7:12]
        r = types.SimpleNamespace(**dict(zip(scratch, refs[12:])))
        me_seq = lax.axis_index("seq")
        me = lax.axis_index("tensor")
        core = lax.rem(me, 2)
        chip = lax.div(me, 2)
        partner = me + 1 - 2 * core
        own_rows = window(me, rows)
        own_tokens = window(me_seq, tokens)
        own_columns = window(me_seq, HEAD_DIM)

        barrier = pltpu.get_barrier_semaphore()
        for step in range(1, tensor_count):
            pl.semaphore_signal(
                barrier,
                inc=1,
                device_id={"tensor": lax.rem(me + step, tensor_count)},
                device_id_type=MESH,
            )
        for mask in order:
            pl.semaphore_signal(
                barrier,
                inc=1,
                device_id={"seq": flipped(me_seq, mask, bits)},
                device_id_type=MESH,
            )

        def load(index, source, target):
            return pltpu.make_async_copy(source, target, r.load_sem.at[index])

        loads = [
            load(0, point_hbm, r.point),
            load(1, gain_hbm, r.gain),
            load(2, incoming_hbm, r.pieces.at[1, own_rows, :]),
            load(3, layout_hbm, r.layout),
            load(4, cosine_hbm, r.cosine),
            load(5, sine_hbm, r.sine),
        ]
        for copy in loads:
            copy.start()

        def weight_load(item, chunk):
            source = (wq_hbm, wk_hbm, wv_hbm, wo_hbm)[item]
            target = (r.wq, r.wk, r.wv, r.wo)[item]
            place = window(chunk, part)
            if item < 3:
                source, target = source.at[place, :], target.at[place, :]
            else:
                source, target = source.at[:, place], target.at[:, place]
            return pltpu.make_async_copy(source, target, r.weight_sem.at[item, chunk])

        for chunk in range(CHUNKS):
            for item in range(3):
                weight_load(item, chunk).start()
        for chunk in range(CHUNKS):
            weight_load(3, chunk).start()

        def remote(source, target, send, recv, axis, peer):
            return pltpu.make_async_remote_copy(
                src_ref=source,
                dst_ref=target,
                send_sem=send,
                recv_sem=recv,
                device_id={axis: peer},
                device_id_type=MESH,
            )

        def gather_copy(item, chunk, slot, origin, peer):
            block = r.pieces.at[item, window(origin, rows), window(chunk, part)]
            return remote(
                block,
                block,
                r.gather_send.at[item, chunk, slot],
                r.gather_recv.at[item, chunk, slot],
                "tensor",
                peer,
            )

        def gather_far(item, chunk, step):
            peer = 2 * lax.rem(chip + step, chips) + core
            return gather_copy(item, chunk, step, me, peer)

        def gather_near(item, chunk):
            return gather_copy(item, chunk, 0, me, partner)

        def gather_pass(item, chunk, step):
            origin = 2 * lax.rem(chip + chips - step, chips) + core
            return gather_copy(item, chunk, chips - 1 + step, origin, partner)

        def gather_start(item):
            for chunk in range(CHUNKS):
                for step in range(1, chips):
                    gather_far(item, chunk, step).start()
                gather_near(item, chunk).start()

        def gather_relay(item, chunk):
            for step in range(1, chips):
                gather_far(item, chunk, step).wait_recv()
                gather_pass(item, chunk, step).start()

        def gather_ready(item, chunk):
            gather_near(item, chunk).wait_recv()
            for step in range(1, chips):
                gather_pass(item, chunk, step).wait_recv()

        def gather_drain(item):
            def drain(chunk, carry):
                gather_near(item, chunk).wait_send()
                for step in range(1, chips):
                    gather_far(item, chunk, step).wait_send()
                    gather_pass(item, chunk, step).wait_send()
                return carry

            lax.fori_loop(0, CHUNKS, drain, 0)

        def gather_each(item, use):
            gather_relay(item, 0)

            def body(chunk, carry):
                @pl.when(chunk + 1 < CHUNKS)
                def _():
                    gather_relay(item, chunk + 1)

                gather_ready(item, chunk)
                use(chunk)
                return carry

            lax.fori_loop(0, CHUNKS, body, 0)

        def heads_copy(item, mask):
            return remote(
                r.heads_out.at[item, mask],
                r.heads_in.at[item, own_tokens, :],
                r.heads_send.at[item, mask],
                r.heads_recv.at[item, mask],
                "seq",
                flipped(me_seq, mask, bits),
            )

        def heads_start(item, slot, turn):
            for mask in order + [0]:
                columns = window(flipped(me_seq, mask, bits), HEAD_DIM)
                values = r.acc[slot, :, columns]
                if turn:
                    values = (
                        values * r.cosine[own_tokens, :]
                        + pltpu.roll(values, HEAD_DIM // 2, 1) * r.sine[own_tokens, :]
                    )
                if mask:
                    r.heads_out[item, mask] = values.astype(low)
                else:
                    r.heads_in[item, own_tokens, :] = values.astype(low)
            for mask in order:
                heads_copy(item, mask).start()

        def heads_ready(item):
            for mask in order:
                heads_copy(item, mask).wait_recv()

        def grads_copy(item, mask):
            peer = flipped(me_seq, mask, bits)
            return remote(
                r.grads_out.at[item, window(peer, tokens), :],
                r.grads_in.at[item, :, own_columns],
                r.grads_send.at[item, mask],
                r.grads_recv.at[item, mask],
                "seq",
                peer,
            )

        def grads_start(item):
            for mask in order:
                grads_copy(item, mask).start()
            r.grads_in[item, :, own_columns] = r.grads_out[item, own_tokens, :]

        def grads_ready(item):
            for mask in order:
                grads_copy(item, mask).wait_recv()

        def hand_copy(term, step, chunk):
            place = window(chunk, part)
            item = term * chips + step
            return remote(
                r.hand_out.at[item, :, place],
                r.hand_in.at[item, :, place],
                r.hand_send.at[item, chunk],
                r.hand_recv.at[item, chunk],
                "tensor",
                partner,
            )

        def far_copy(term, step, chunk):
            place = window(chunk, part)
            item = term * chips + step
            return remote(
                r.far_out.at[item, :, place],
                r.far_in.at[item, :, place],
                r.far_send.at[item, chunk],
                r.far_recv.at[item, chunk],
                "tensor",
                2 * lax.rem(chip + step, chips) + core,
            )

        def near_copy(step, chunk):
            place = window(chunk, gain_part)
            return remote(
                r.gain_own.at[place, :],
                r.gain_near.at[step, place, :],
                r.near_send.at[step, chunk],
                r.near_recv.at[step, chunk],
                "tensor",
                lax.rem(me + step, tensor_count),
            )

        def wide_copy(mask, chunk):
            place = window(chunk, gain_part)
            return remote(
                r.gain_mid.at[place, :],
                r.gain_far.at[mask, place, :],
                r.wide_send.at[mask, chunk],
                r.wide_recv.at[mask, chunk],
                "seq",
                flipped(me_seq, mask, bits),
            )

        loads[0].wait()
        loads[1].wait()
        point = r.point[...].astype(full)
        inv_rms = lax.rsqrt(jnp.mean(point * point, axis=1, keepdims=True) + EPS)
        r.scaled[...] = point * inv_rms
        r.pieces[0, own_rows, :] = (r.gain[...] * r.scaled[...]).astype(low)
        loads[2].wait()
        pl.semaphore_wait(barrier, tensor_count - 1 + seq_count - 1)
        gather_start(0)
        gather_start(1)

        loads[3].wait()
        spread = (
            lax.broadcasted_iota(jnp.int32, (blocks, length), 1) // BLK
            == lax.broadcasted_iota(jnp.int32, (blocks, length), 0)
        )
        chosen = product(
            jnp.where(r.layout[...] > 0, 1.0, 0.0).astype(low),
            jnp.where(spread, 1.0, 0.0).astype(low),
            1,
            0,
        )
        earlier = (
            lax.broadcasted_iota(jnp.int32, (blocks, length), 1) // BLK
            < lax.broadcasted_iota(jnp.int32, (blocks, length), 0)
        )
        r.bias[...] = jnp.where(earlier & (chosen > 0.5), 0.0, MASKED)
        r.acc[...] = jnp.zeros(r.acc.shape, full)

        def project(chunk):
            place = window(chunk, part)
            for item, weight in enumerate((r.wq, r.wk, r.wv)):
                weight_load(item, chunk).wait()
                r.acc[item] += product(r.pieces[0, :, place], weight[place, :], 1, 0)

        gather_each(0, project)
        loads[4].wait()
        loads[5].wait()
        heads_start(0, 0, True)
        heads_start(1, 1, True)
        heads_start(2, 2, False)

        def pull(item):
            def use(chunk):
                if item == 1:
                    weight_load(3, chunk).wait()
                place = window(chunk, part)
                r.acc[3] += product(r.pieces[item, :, place], r.wo[:, place], 1, 1)

            return use

        gather_each(1, pull(1))
        heads_start(3, 3, False)

        group = 2 if seq_count % 2 == 0 else 1
        heads_ready(0)
        heads_ready(1)
        sub = tokens // BLK

        def forward(base):
            span = (base + group) * tokens

            def body(step, carry):
                place = window(base + step, tokens)
                scores = product(r.heads_in[0, place, :], r.heads_in[1, :span, :], 1, 1) * score_scale
                query_at = (base + step) * tokens + lax.broadcasted_iota(jnp.int32, (tokens, span), 0)
                key_at = lax.broadcasted_iota(jnp.int32, (tokens, span), 1)
                same = (query_at // BLK == key_at // BLK) & (key_at <= query_at)
                bias = jnp.concatenate(
                    [
                        jnp.broadcast_to(r.bias[pl.ds((base + step) * sub + line, 1), :span], (BLK, span))
                        for line in range(sub)
                    ],
                    axis=0,
                )
                scores = scores + jnp.where(same, 0.0, bias)
                top = jnp.max(scores, axis=1, keepdims=True)
                weight = jnp.exp(scores - top)
                r.probs[place, :span] = (weight / jnp.sum(weight, axis=1, keepdims=True)).astype(low)
                return carry

            lax.fori_loop(0, group, body, 0)

        for base in range(0, seq_count, group):
            forward(base)

        def turned_back(values, place):
            return (
                values * r.cosine[place, :]
                - pltpu.roll(values, HEAD_DIM // 2, 1) * r.sine[place, :]
            ).astype(low)

        def backward(term):
            r.key_acc[...] = jnp.zeros(r.key_acc.shape, full)
            r.value_acc[...] = jnp.zeros(r.value_acc.shape, full)

            def at(base):
                span = (base + group) * tokens

                def body(step, carry):
                    place = window(base + group - 1 - step, tokens)
                    probs = r.probs[place, :span]
                    grad_low = r.heads_in[3 + term, place, :]
                    grad_probs = product(grad_low, r.heads_in[2, :span, :], 1, 1)
                    wide = probs.astype(full)
                    delta = jnp.sum(wide * grad_probs, axis=1, keepdims=True)
                    grad_scores = (wide * (grad_probs - delta)).astype(low)
                    grad_query = product(grad_scores, r.heads_in[1, :span, :], 1, 0) * score_scale
                    r.grads_out[3 * term, place, :] = turned_back(grad_query, place)
                    r.key_acc[:span, :] += product(grad_scores, r.heads_in[0, place, :], 0, 0)
                    r.value_acc[:span, :] += product(probs, grad_low, 0, 0)
                    return carry

                lax.fori_loop(0, group, body, 0)

            for base in reversed(range(0, seq_count, group)):
                at(base)
            r.grads_out[3 * term + 2] = r.value_acc[...].astype(low)
            grads_start(3 * term + 2)
            r.grads_out[3 * term + 1] = turned_back(r.key_acc[...] * score_scale, slice(None))
            grads_start(3 * term + 1)
            grads_start(3 * term)

        def hand_on(term, chunk):
            place = window(chunk, part)
            for step in range(chips):
                hand_copy(term, step, chunk).wait_recv()
                owner = 2 * lax.rem(chip + step, chips) + core
                pair = r.total[window(owner, rows), place] + r.hand_in[
                    term * chips + step, :, place
                ].astype(full)
                if step:
                    r.far_out[term * chips + step, :, place] = pair.astype(low)
                    far_copy(term, step, chunk).start()
                else:
                    r.normed_grad[:, place] = pair

        def push(term):
            for item, weight in ((2, r.wv), (1, r.wk)):
                grads_ready(3 * term + item)

                def body(chunk, carry):
                    place = window(chunk, part)
                    value = product(r.grads_in[3 * term + item], weight[place, :], 1, 1)
                    if item == 1:
                        value = value + r.total[:, place]
                    r.total[:, place] = value
                    return carry

                lax.fori_loop(0, CHUNKS, body, 0)
            grads_ready(3 * term)

            def last(chunk, carry):
                place = window(chunk, part)
                r.total[:, place] += product(r.grads_in[3 * term], r.wq[place, :], 1, 1)
                for step in range(chips):
                    other = 2 * lax.rem(chip + step, chips) + 1 - core
                    r.hand_out[term * chips + step, :, place] = r.total[
                        window(other, rows), place
                    ].astype(low)
                for step in range(chips):
                    hand_copy(term, step, chunk).start()

                @pl.when(chunk > 0)
                def _():
                    hand_on(term, chunk - 1)

                return carry

            lax.fori_loop(0, CHUNKS, last, 0)
            hand_on(term, CHUNKS - 1)

        def near_sum(chunk):
            for step in range(1, tensor_count):
                near_copy(step, chunk).wait_recv()
            place = window(chunk, gain_part)
            value = r.gain_own[place, :]
            for step in range(1, tensor_count):
                value = value + r.gain_near[step, place, :]
            r.gain_mid[place, :] = value
            for mask in order:
                wide_copy(mask, chunk).start()

        for term in range(ITERS):
            if term:
                r.acc[3] = jnp.zeros((tokens, head_width), full)
                gather_start(1 + term)
                gather_each(1 + term, pull(1 + term))
                heads_start(3 + term, 3, False)
            else:
                heads_ready(2)
            heads_ready(3 + term)
            backward(term)
            push(term)
            final = term == ITERS - 1
            for chunk in range(CHUNKS):
                place = slice(chunk * part, (chunk + 1) * part)
                value = r.normed_grad[:, place]
                for step in range(1, chips):
                    far_copy(term, step, chunk).wait_recv()
                    value = value + r.far_in[term * chips + step, :, place].astype(full)
                r.normed_grad[:, place] = value
                gain_term = jnp.sum(value * r.scaled[:, place], axis=0, keepdims=True)
                if term:
                    gain_term = gain_term + r.gain_sum[:, place]
                if not final:
                    r.gain_sum[:, place] = gain_term
                    continue
                for line in range(gain_part):
                    r.gain_own[chunk * gain_part + line : chunk * gain_part + line + 1, :] = gain_term[
                        :, line * HEAD_DIM : (line + 1) * HEAD_DIM
                    ]
                for step in range(1, tensor_count):
                    near_copy(step, chunk).start()
                if chunk:
                    near_sum(chunk - 1)
            weighted = r.gain[...] * r.normed_grad[...]
            inner = jnp.sum(weighted * r.scaled[...], axis=1, keepdims=True)
            cotangent = inv_rms * (weighted - r.scaled[...] * (inner / width))
            if term == 0:
                r.adjoint[...] = r.pieces[1, own_rows, :].astype(full) + cotangent
            else:
                r.adjoint[...] += cotangent
            if not final:
                r.pieces[2 + term, own_rows, :] = cotangent.astype(low)

        out_copy = load(6, r.adjoint, adjoint_hbm)
        out_copy.start()
        near_sum(CHUNKS - 1)
        for item in range(1 + ITERS):
            gather_drain(item)
        for item in range(3 + ITERS):
            for mask in order:
                heads_copy(item, mask).wait_send()
        for item in range(3 * ITERS):
            for mask in order:
                grads_copy(item, mask).wait_send()
        for chunk in range(CHUNKS):
            for term in range(ITERS):
                for step in range(chips):
                    hand_copy(term, step, chunk).wait_send()
                    if step:
                        far_copy(term, step, chunk).wait_send()
            for step in range(1, tensor_count):
                near_copy(step, chunk).wait_send()
        for chunk in range(CHUNKS):
            for mask in order:
                wide_copy(mask, chunk).wait()
        value = r.gain_mid[...]
        for mask in order:
            value = value + r.gain_far[mask]
        r.gain_out[...] = value * length ** (-0.5)
        out_copy.wait()
        gain_copy = load(0, r.gain_out, gain_out_hbm)
        gain_copy.start()
        gain_copy.wait()

    anywhere = pl.BlockSpec(memory_space=pl.ANY)
    adjoint, gain_grad = pl.pallas_call(
        kernel,
        out_shape=[
            jax.ShapeDtypeStruct((rows, width), full),
            jax.ShapeDtypeStruct((gain_rows, HEAD_DIM), full),
        ],
        in_specs=[anywhere] * 10,
        out_specs=[anywhere] * 2,
        scratch_shapes=list(scratch.values()),
        compiler_params=pltpu.CompilerParams(
            collective_id=0, has_side_effects=True, vmem_limit_bytes=67043328
        ),
    )(
        fixed_point,
        incoming,
        norm_gain.reshape(1, width),
        query_weight,
        key_weight,
        value_weight,
        out_weight,
        layout,
        jnp.asarray(cosine),
        jnp.asarray(sine),
    )
    return adjoint, gain_grad.reshape(width)


def solution(mesh):
    in_specs = (
        P(("seq", "tensor"), None),
        P(("seq", "tensor"), None),
        P(),
        P(None, "tensor"),
        P(None, "tensor"),
        P(None, "tensor"),
        P("tensor", None),
        P(),
    )
    out_specs = (P(("seq", "tensor"), None), P())
    seq, tensor = mesh.shape["seq"], mesh.shape["tensor"]

    def body(*arrays):
        heads = arrays[3].shape[1] * tensor // HEAD_DIM
        tokens = arrays[0].shape[0] * tensor
        fits = (
            tensor % 2 == 0
            and seq & (seq - 1) == 0
            and heads == seq * tensor
            and tokens % 128 == 0
            and arrays[0].shape[0] % 16 == 0
            and arrays[0].shape[1] % (8 * HEAD_DIM * CHUNKS) == 0
        )
        return (fused_body if fits else ring_body)(*arrays)

    return jax.shard_map(body, mesh=mesh, in_specs=in_specs, out_specs=out_specs, check_vma=False)
```

time: 212 us -> 146 us (0.69); the launches traced: 210 us -> 146 us
  matrix products: 54.2 us -> 0 us
  other arithmetic: 10.6 us -> 0 us
  Pallas kernels: 138 us -> 142 us
  local copies, waits for them, and re-layouts: 5.32 us -> 3.19 us
    dot_general x22 -> x0, matrix products: 54.2 us -> none  [the longest x18 49.4 us: product(): lax.dot_general(left, right, (((left_dim,), (right_dim,)), ((), ())), pre...]
    pallas_call x10 -> x1, Pallas kernels: 138 us -> 142 us  [fused_body(): pl.pallas_call(kernel, out_shape=[jax.ShapeDtypeStruct((rows, width), ful...]
    convert_element_type x7 -> x0, other arithmetic: 3.39 us -> none  [the longest x1 1.08 us: head_body(): normed = (norm_gain * scaled).astype(jnp.bfloat16)]
    reduce_sum x7 -> x0, other arithmetic: 2.55 us -> none  [the longest x1 1.11 us: head_body(): inv_rms = lax.rsqrt(jnp.mean(point * point, axis=1, keepdims=True) + EPS)]
    unnamed x51 -> x2, local copies, waits for them, and re-layouts: 5.28 us -> 3.19 us
where the time goes in v1:
time: 146 us
  Pallas kernels  142 us (97%)
  local copies, waits for them, and re-layouts  3.19 us (2%)
    pallas_call x1, Pallas kernels, fused_body(): pl.pallas_call(kernel, out_shape=[jax.ShapeDtypeStruct((rows, width), ful...  142 us
    unnamed x2, local copies, waits for them, and re-layouts  3.19 us

profile of v1, /device:TPU:0, one launch (start us, length us, event | category | flops | bytes accessed | tf_op | source)
XLA Modules:
  0.0 145.9 jit_solution(7108149082439774117)
XLA Ops:
  0.6 142.1 %shard_map.113 = (f32[32,4096]{1,0:T(8,128)}, f32[32,128]{1,0:T(8,128)}) custom-call(bf16[32,4096]{1,0:T(8,128)(2,1)} %refs_0_.1, bf16[32,4096]{1,0:T(8,128)(2,1)} %refs_1_.1, f32[1,4096]{1,0:T(1,128)} %bitcast.2, bf16[4096,1024]{1,0:T(8,128)(2,1)} %refs_3_.1, bf16[4096,1024]{1,0:T(8,128)(2,1)} %refs_4_.1, bf16[4096,1024]{1,0:T(8,128)(2,1)} %refs_5_.1, ...), custom_call_target="tpu_custom_call" | custom-call | tf_op jit(solution)/shard_map/pallas_call | solution.py:770
  142.7 1.9 %copy.14 = f32[32,4096]{1,0:T(8,128)} copy(f32[32,4096]{1,0:T(8,128)} %get-tuple-element.8) | data formatting | bytes 1048576
  144.6 1.3 copy.15

commit v2 on v1

--- a/solution.py
+++ b/solution.py
@@ -229,26 +229,25 @@
     order = list(range(seq_count - 1, 0, -1))
     low, full = jnp.bfloat16, jnp.float32
     dma = pltpu.SemaphoreType.DMA
-    hops = 2 * chips - 1
     scratch = {
         "wq": pltpu.VMEM((width, head_width), low),
         "wk": pltpu.VMEM((width, head_width), low),
         "wv": pltpu.VMEM((width, head_width), low),
         "wo": pltpu.VMEM((head_width, width), low),
-        "point": pltpu.VMEM((rows, width), low),
+        "point": pltpu.VMEM((chips, rows, width), low),
         "gain": pltpu.VMEM((1, width), full),
         "layout": pltpu.VMEM(layout.shape, jnp.int32),
         "cosine": pltpu.VMEM((length, HEAD_DIM), full),
         "sine": pltpu.VMEM((length, HEAD_DIM), full),
         "bias": pltpu.VMEM((blocks, length), full),
-        "scaled": pltpu.VMEM((rows, width), full),
+        "scaled": pltpu.VMEM((chips, rows, width), full),
         "pieces": pltpu.VMEM((1 + ITERS, tokens, width), low),
         "acc": pltpu.VMEM((4, tokens, head_width), full),
         "heads_out": pltpu.VMEM((3 + ITERS, seq_count, tokens, HEAD_DIM), low),
         "heads_in": pltpu.VMEM((3 + ITERS, length, HEAD_DIM), low),
         "probs": pltpu.VMEM((length, length), low),
         "key_acc": pltpu.VMEM((length, HEAD_DIM), full),
-        "value_acc": pltpu.VMEM((length, HEAD_DIM), full),
+        "probs_turned": pltpu.VMEM((length, length), low),
         "grads_out": pltpu.VMEM((3 * ITERS, length, HEAD_DIM), low),
         "grads_in": pltpu.VMEM((3 * ITERS, tokens, head_width), low),
         "total": pltpu.VMEM((tokens, width), full),
@@ -257,34 +256,35 @@
         "far_out": pltpu.VMEM((ITERS * chips, rows, width), low),
         "far_in": pltpu.VMEM((ITERS * chips, rows, width), low),
         "normed_grad": pltpu.VMEM((rows, width), full),
-        "adjoint": pltpu.VMEM((rows, width), full),
         "gain_sum": pltpu.VMEM((1, width), full),
         "gain_own": pltpu.VMEM((gain_rows, HEAD_DIM), full),
         "gain_near": pltpu.VMEM((tensor_count, gain_rows, HEAD_DIM), full),
         "gain_mid": pltpu.VMEM((gain_rows, HEAD_DIM), full),
         "gain_far": pltpu.VMEM((seq_count, gain_rows, HEAD_DIM), full),
-        "gain_out": pltpu.VMEM((gain_rows, HEAD_DIM), full),
-        "load_sem": dma((7,)),
-        "weight_sem": dma((4, CHUNKS)),
-        "gather_send": dma((1 + ITERS, CHUNKS, hops)),
-        "gather_recv": dma((1 + ITERS, CHUNKS, hops)),
-        "heads_send": dma((3 + ITERS, seq_count)),
-        "heads_recv": dma((3 + ITERS, seq_count)),
-        "grads_send": dma((3 * ITERS, seq_count)),
-        "grads_recv": dma((3 * ITERS, seq_count)),
-        "hand_send": dma((ITERS * chips, CHUNKS)),
-        "hand_recv": dma((ITERS * chips, CHUNKS)),
-        "far_send": dma((ITERS * chips, CHUNKS)),
-        "far_recv": dma((ITERS * chips, CHUNKS)),
-        "near_send": dma((tensor_count, CHUNKS)),
-        "near_recv": dma((tensor_count, CHUNKS)),
-        "wide_send": dma((seq_count, CHUNKS)),
-        "wide_recv": dma((seq_count, CHUNKS)),
+        "load_sem": dma((6,)),
+        "weight_sem": dma((CHUNKS + 1,)),
+        "gather_send": dma((1 + ITERS,)),
+        "gather_far": dma((1 + ITERS, CHUNKS * (chips - 1))),
+        "gather_near": dma((1 + ITERS, CHUNKS)),
+        "heads_send": dma((3 + ITERS,)),
+        "heads_recv": dma((3 + ITERS,)),
+        "grads_send": dma((3 * ITERS,)),
+        "grads_recv": dma((3 * ITERS,)),
+        "hand_send": dma((ITERS,)),
+        "hand_recv": dma((ITERS, CHUNKS)),
+        "far_send": dma((ITERS,)),
+        "far_recv": dma((ITERS, CHUNKS)),
+        "point_send": dma((1,)),
+        "point_recv": dma((1,)),
+        "near_send": dma((1,)),
+        "near_recv": dma((1,)),
+        "wide_send": dma((1,)),
+        "wide_recv": dma((1,)),
     }
 
     def kernel(*refs):
         point_hbm, incoming_hbm, gain_hbm, wq_hbm, wk_hbm, wv_hbm, wo_hbm = refs[:7]
-        layout_hbm, cosine_hbm, sine_hbm, adjoint_hbm, gain_out_hbm = refs[7:12]
+        layout_hbm, cosine_hbm, sine_hbm, adjoint_out, gain_out = refs[7:12]
         r = types.SimpleNamespace(**dict(zip(scratch, refs[12:])))
         me_seq = lax.axis_index("seq")
         me = lax.axis_index("tensor")
@@ -315,31 +315,31 @@
             return pltpu.make_async_copy(source, target, r.load_sem.at[index])
 
         loads = [
-            load(0, point_hbm, r.point),
+            load(0, point_hbm, r.point.at[0]),
             load(1, gain_hbm, r.gain),
             load(2, incoming_hbm, r.pieces.at[1, own_rows, :]),
             load(3, layout_hbm, r.layout),
             load(4, cosine_hbm, r.cosine),
             load(5, sine_hbm, r.sine),
         ]
-        for copy in loads:
-            copy.start()
+        for index in (0, 1, 2, 3):
+            loads[index].start()
 
         def weight_load(item, chunk):
-            source = (wq_hbm, wk_hbm, wv_hbm, wo_hbm)[item]
-            target = (r.wq, r.wk, r.wv, r.wo)[item]
+            source = (wq_hbm, wk_hbm, wv_hbm)[item]
+            target = (r.wq, r.wk, r.wv)[item]
             place = window(chunk, part)
-            if item < 3:
-                source, target = source.at[place, :], target.at[place, :]
-            else:
-                source, target = source.at[:, place], target.at[:, place]
-            return pltpu.make_async_copy(source, target, r.weight_sem.at[item, chunk])
-
-        for chunk in range(CHUNKS):
-            for item in range(3):
-                weight_load(item, chunk).start()
-        for chunk in range(CHUNKS):
-            weight_load(3, chunk).start()
+            return pltpu.make_async_copy(
+                source.at[place, :], target.at[place, :], r.weight_sem.at[chunk]
+            )
+
+        def weight_ready(chunk):
+            whole = pl.ds(0, 3 * part)
+            pltpu.make_async_copy(
+                wq_hbm.at[whole, :], r.wq.at[whole, :], r.weight_sem.at[chunk]
+            ).wait()
+
+        out_load = pltpu.make_async_copy(wo_hbm, r.wo, r.weight_sem.at[CHUNKS])
 
         def remote(source, target, send, recv, axis, peer):
             return pltpu.make_async_remote_copy(
@@ -351,27 +351,21 @@
                 device_id_type=MESH,
             )
 
-        def gather_copy(item, chunk, slot, origin, peer):
+        def gather_copy(item, chunk, recv, origin, peer):
             block = r.pieces.at[item, window(origin, rows), window(chunk, part)]
-            return remote(
-                block,
-                block,
-                r.gather_send.at[item, chunk, slot],
-                r.gather_recv.at[item, chunk, slot],
-                "tensor",
-                peer,
-            )
+            return remote(block, block, r.gather_send.at[item], recv, "tensor", peer)
 
         def gather_far(item, chunk, step):
             peer = 2 * lax.rem(chip + step, chips) + core
-            return gather_copy(item, chunk, step, me, peer)
+            recv = r.gather_far.at[item, chunk * (chips - 1) + step - 1]
+            return gather_copy(item, chunk, recv, me, peer)
 
         def gather_near(item, chunk):
-            return gather_copy(item, chunk, 0, me, partner)
+            return gather_copy(item, chunk, r.gather_near.at[item, chunk], me, partner)
 
         def gather_pass(item, chunk, step):
             origin = 2 * lax.rem(chip + chips - step, chips) + core
-            return gather_copy(item, chunk, chips - 1 + step, origin, partner)
+            return gather_copy(item, chunk, r.gather_near.at[item, chunk], origin, partner)
 
         def gather_start(item):
             for chunk in range(CHUNKS):
@@ -385,21 +379,16 @@
                 gather_pass(item, chunk, step).start()
 
         def gather_ready(item, chunk):
-            gather_near(item, chunk).wait_recv()
-            for step in range(1, chips):
-                gather_pass(item, chunk, step).wait_recv()
+            block = r.pieces.at[item, pl.ds(0, chips * rows), window(chunk, part)]
+            send, recv = r.gather_send.at[item], r.gather_near.at[item, chunk]
+            remote(block, block, send, recv, "tensor", partner).wait_recv()
 
         def gather_drain(item):
-            def drain(chunk, carry):
-                gather_near(item, chunk).wait_send()
-                for step in range(1, chips):
-                    gather_far(item, chunk, step).wait_send()
-                    gather_pass(item, chunk, step).wait_send()
-                return carry
-
-            lax.fori_loop(0, CHUNKS, drain, 0)
-
-        def gather_each(item, use):
+            block = r.pieces.at[item, pl.ds(0, (2 * chips - 1) * rows), :]
+            send, recv = r.gather_send.at[item], r.gather_near.at[item, 0]
+            remote(block, block, send, recv, "tensor", partner).wait_send()
+
+        def gather_each(item, use, after=None):
             gather_relay(item, 0)
 
             def body(chunk, carry):
@@ -407,18 +396,34 @@
                 def _():
                     gather_relay(item, chunk + 1)
 
+                if after is not None:
+
+                    @pl.when(chunk + 2 == CHUNKS)
+                    def _():
+                        after()
+
                 gather_ready(item, chunk)
                 use(chunk)
                 return carry
 
             lax.fori_loop(0, CHUNKS, body, 0)
+
+        def point_copy(step):
+            return remote(
+                r.point.at[0],
+                r.point.at[chips - step],
+                r.point_send.at[0],
+                r.point_recv.at[0],
+                "tensor",
+                2 * lax.rem(chip + step, chips) + core,
+            )
 
         def heads_copy(item, mask):
             return remote(
                 r.heads_out.at[item, mask],
                 r.heads_in.at[item, own_tokens, :],
-                r.heads_send.at[item, mask],
-                r.heads_recv.at[item, mask],
+                r.heads_send.at[item],
+                r.heads_recv.at[item],
                 "seq",
                 flipped(me_seq, mask, bits),
             )
@@ -440,16 +445,22 @@
                 heads_copy(item, mask).start()
 
         def heads_ready(item):
-            for mask in order:
-                heads_copy(item, mask).wait_recv()
+            block = r.heads_in.at[item, pl.ds(0, (seq_count - 1) * tokens), :]
+            send, recv = r.heads_send.at[item], r.heads_recv.at[item]
+            remote(block, block, send, recv, "seq", flipped(me_seq, 1, bits)).wait_recv()
+
+        def heads_drain(item):
+            block = r.heads_out.at[item, pl.ds(1, seq_count - 1)]
+            send, recv = r.heads_send.at[item], r.heads_recv.at[item]
+            remote(block, block, send, recv, "seq", flipped(me_seq, 1, bits)).wait_send()
 
         def grads_copy(item, mask):
             peer = flipped(me_seq, mask, bits)
             return remote(
                 r.grads_out.at[item, window(peer, tokens), :],
                 r.grads_in.at[item, :, own_columns],
-                r.grads_send.at[item, mask],
-                r.grads_recv.at[item, mask],
+                r.grads_send.at[item],
+                r.grads_recv.at[item],
                 "seq",
                 peer,
             )
@@ -460,8 +471,14 @@
             r.grads_in[item, :, own_columns] = r.grads_out[item, own_tokens, :]
 
         def grads_ready(item):
-            for mask in order:
-                grads_copy(item, mask).wait_recv()
+            block = r.grads_in.at[item, :, pl.ds(0, (seq_count - 1) * HEAD_DIM)]
+            send, recv = r.grads_send.at[item], r.grads_recv.at[item]
+            remote(block, block, send, recv, "seq", flipped(me_seq, 1, bits)).wait_recv()
+
+        def grads_drain(item):
+            block = r.grads_out.at[item, pl.ds(0, (seq_count - 1) * tokens), :]
+            send, recv = r.grads_send.at[item], r.grads_recv.at[item]
+            remote(block, block, send, recv, "seq", flipped(me_seq, 1, bits)).wait_send()
 
         def hand_copy(term, step, chunk):
             place = window(chunk, part)
@@ -469,8 +486,8 @@
             return remote(
                 r.hand_out.at[item, :, place],
                 r.hand_in.at[item, :, place],
-                r.hand_send.at[item, chunk],
-                r.hand_recv.at[item, chunk],
+                r.hand_send.at[term],
+                r.hand_recv.at[term, chunk],
                 "tensor",
                 partner,
             )
@@ -481,44 +498,70 @@
             return remote(
                 r.far_out.at[item, :, place],
                 r.far_in.at[item, :, place],
-                r.far_send.at[item, chunk],
-                r.far_recv.at[item, chunk],
+                r.far_send.at[term],
+                r.far_recv.at[term, chunk],
                 "tensor",
                 2 * lax.rem(chip + step, chips) + core,
             )
 
-        def near_copy(step, chunk):
+        def hand_ready(term, chunk):
+            block = r.hand_in.at[pl.ds(term * chips, chips), :, window(chunk, part)]
+            send, recv = r.hand_send.at[term], r.hand_recv.at[term, chunk]
+            remote(block, block, send, recv, "tensor", partner).wait_recv()
+
+        def far_ready(term, chunk):
+            block = r.far_in.at[pl.ds(term * chips + 1, chips - 1), :, window(chunk, part)]
+            send, recv = r.far_send.at[term], r.far_recv.at[term, chunk]
+            remote(block, block, send, recv, "tensor", partner).wait_recv()
+
+        def reduce_drain(term):
+            block = r.hand_out.at[pl.ds(term * chips, chips)]
+            send, recv = r.hand_send.at[term], r.hand_recv.at[term, 0]
+            remote(block, block, send, recv, "tensor", partner).wait_send()
+            block = r.far_out.at[pl.ds(term * chips + 1, chips - 1)]
+            send, recv = r.far_send.at[term], r.far_recv.at[term, 0]
+            remote(block, block, send, recv, "tensor", partner).wait_send()
+
+        def wide_copy(mask, chunk):
             place = window(chunk, gain_part)
             return remote(
                 r.gain_own.at[place, :],
-                r.gain_near.at[step, place, :],
-                r.near_send.at[step, chunk],
-                r.near_recv.at[step, chunk],
+                r.gain_far.at[mask, place, :],
+                r.wide_send.at[0],
+                r.wide_recv.at[0],
+                "seq",
+                flipped(me_seq, mask, bits),
+            )
+
+        def near_copy(step):
+            return remote(
+                r.gain_mid,
+                r.gain_near.at[step],
+                r.near_send.at[0],
+                r.near_recv.at[0],
                 "tensor",
                 lax.rem(me + step, tensor_count),
             )
 
-        def wide_copy(mask, chunk):
-            place = window(chunk, gain_part)
-            return remote(
-                r.gain_mid.at[place, :],
-                r.gain_far.at[mask, place, :],
-                r.wide_send.at[mask, chunk],
-                r.wide_recv.at[mask, chunk],
-                "seq",
-                flipped(me_seq, mask, bits),
-            )
-
-        loads[0].wait()
-        loads[1].wait()
-        point = r.point[...].astype(full)
-        inv_rms = lax.rsqrt(jnp.mean(point * point, axis=1, keepdims=True) + EPS)
-        r.scaled[...] = point * inv_rms
-        r.pieces[0, own_rows, :] = (r.gain[...] * r.scaled[...]).astype(low)
-        loads[2].wait()
+        for copy in loads[:3]:
+            copy.wait()
+        for chunk in range(CHUNKS):
+            for item in range(3):
+                weight_load(item, chunk).start()
+        out_load.start()
+        for copy in loads[4:]:
+            copy.start()
+
+        def scale(step):
+            point = r.point[step].astype(full)
+            inv_rms = lax.rsqrt(jnp.mean(point * point, axis=1, keepdims=True) + EPS)
+            r.scaled[step] = point * inv_rms
+            return inv_rms
+
+        inv_rms = scale(0)
+        r.pieces[0, own_rows, :] = (r.gain[...] * r.scaled[0]).astype(low)
         pl.semaphore_wait(barrier, tensor_count - 1 + seq_count - 1)
         gather_start(0)
-        gather_start(1)
 
         loads[3].wait()
         spread = (
@@ -540,11 +583,11 @@
 
         def project(chunk):
             place = window(chunk, part)
+            weight_ready(chunk)
             for item, weight in enumerate((r.wq, r.wk, r.wv)):
-                weight_load(item, chunk).wait()
                 r.acc[item] += product(r.pieces[0, :, place], weight[place, :], 1, 0)
 
-        gather_each(0, project)
+        gather_each(0, project, lambda: gather_start(1))
         loads[4].wait()
         loads[5].wait()
         heads_start(0, 0, True)
@@ -553,15 +596,21 @@
 
         def pull(item):
             def use(chunk):
-                if item == 1:
-                    weight_load(3, chunk).wait()
                 place = window(chunk, part)
                 r.acc[3] += product(r.pieces[item, :, place], r.wo[:, place], 1, 1)
 
             return use
 
+        out_load.wait()
         gather_each(1, pull(1))
         heads_start(3, 3, False)
+        for step in range(1, chips):
+            point_copy(step).start()
+
+        block = r.point.at[pl.ds(1, chips - 1)]
+        remote(block, block, r.point_send.at[0], r.point_recv.at[0], "tensor", partner).wait()
+        for step in range(1, chips):
+            scale(step)
 
         group = 2 if seq_count % 2 == 0 else 1
         heads_ready(0)
@@ -587,7 +636,9 @@
                 scores = scores + jnp.where(same, 0.0, bias)
                 top = jnp.max(scores, axis=1, keepdims=True)
                 weight = jnp.exp(scores - top)
-                r.probs[place, :span] = (weight / jnp.sum(weight, axis=1, keepdims=True)).astype(low)
+                weight = weight / jnp.sum(weight, axis=1, keepdims=True)
+                r.probs[place, :span] = weight.astype(low)
+                r.probs_turned[:span, place] = weight.T.astype(low)
                 return carry
 
             lax.fori_loop(0, group, body, 0)
@@ -603,7 +654,14 @@
 
         def backward(term):
             r.key_acc[...] = jnp.zeros(r.key_acc.shape, full)
-            r.value_acc[...] = jnp.zeros(r.value_acc.shape, full)
+            for base in range(0, seq_count, group):
+                later = slice(base * tokens, length)
+                for step in range(group):
+                    place = slice((base + step) * tokens, (base + step + 1) * tokens)
+                    r.grads_out[3 * term + 2, place, :] = product(
+                        r.probs_turned[place, later], r.heads_in[3 + term, later, :], 1, 0
+                    ).astype(low)
+            grads_start(3 * term + 2)
 
             def at(base):
                 span = (base + group) * tokens
@@ -619,23 +677,21 @@
                     grad_query = product(grad_scores, r.heads_in[1, :span, :], 1, 0) * score_scale
                     r.grads_out[3 * term, place, :] = turned_back(grad_query, place)
                     r.key_acc[:span, :] += product(grad_scores, r.heads_in[0, place, :], 0, 0)
-                    r.value_acc[:span, :] += product(probs, grad_low, 0, 0)
                     return carry
 
                 lax.fori_loop(0, group, body, 0)
 
             for base in reversed(range(0, seq_count, group)):
                 at(base)
-            r.grads_out[3 * term + 2] = r.value_acc[...].astype(low)
-            grads_start(3 * term + 2)
             r.grads_out[3 * term + 1] = turned_back(r.key_acc[...] * score_scale, slice(None))
             grads_start(3 * term + 1)
             grads_start(3 * term)
 
         def hand_on(term, chunk):
             place = window(chunk, part)
+            hand_ready(term, chunk)
+            gain_term = jnp.zeros((1, part), full)
             for step in range(chips):
-                hand_copy(term, step, chunk).wait_recv()
                 owner = 2 * lax.rem(chip + step, chips) + core
                 pair = r.total[window(owner, rows), place] + r.hand_in[
                     term * chips + step, :, place
@@ -645,6 +701,18 @@
                     far_copy(term, step, chunk).start()
                 else:
                     r.normed_grad[:, place] = pair
+                gain_term += jnp.sum(pair * r.scaled[step, :, place], axis=0, keepdims=True)
+            if term:
+                gain_term += r.gain_sum[:, place]
+            if term < ITERS - 1:
+                r.gain_sum[:, place] = gain_term
+                return
+            r.gain_own[window(chunk, gain_part), :] = jnp.concatenate(
+                [gain_term[:, line * HEAD_DIM : (line + 1) * HEAD_DIM] for line in range(gain_part)],
+                axis=0,
+            )
+            for mask in order:
+                wide_copy(mask, chunk).start()
 
         def push(term):
             for item, weight in ((2, r.wv), (1, r.wk)):
@@ -680,17 +748,6 @@
 
             lax.fori_loop(0, CHUNKS, last, 0)
             hand_on(term, CHUNKS - 1)
-
-        def near_sum(chunk):
-            for step in range(1, tensor_count):
-                near_copy(step, chunk).wait_recv()
-            place = window(chunk, gain_part)
-            value = r.gain_own[place, :]
-            for step in range(1, tensor_count):
-                value = value + r.gain_near[step, place, :]
-            r.gain_mid[place, :] = value
-            for mask in order:
-                wide_copy(mask, chunk).start()
 
         for term in range(ITERS):
             if term:
@@ -707,64 +764,43 @@
             for chunk in range(CHUNKS):
                 place = slice(chunk * part, (chunk + 1) * part)
                 value = r.normed_grad[:, place]
+                far_ready(term, chunk)
                 for step in range(1, chips):
-                    far_copy(term, step, chunk).wait_recv()
                     value = value + r.far_in[term * chips + step, :, place].astype(full)
                 r.normed_grad[:, place] = value
-                gain_term = jnp.sum(value * r.scaled[:, place], axis=0, keepdims=True)
-                if term:
-                    gain_term = gain_term + r.gain_sum[:, place]
-                if not final:
-                    r.gain_sum[:, place] = gain_term
-                    continue
-                for line in range(gain_part):
-                    r.gain_own[chunk * gain_part + line : chunk * gain_part + line + 1, :] = gain_term[
-                        :, line * HEAD_DIM : (line + 1) * HEAD_DIM
-                    ]
-                for step in range(1, tensor_count):
-                    near_copy(step, chunk).start()
-                if chunk:
-                    near_sum(chunk - 1)
             weighted = r.gain[...] * r.normed_grad[...]
-            inner = jnp.sum(weighted * r.scaled[...], axis=1, keepdims=True)
-            cotangent = inv_rms * (weighted - r.scaled[...] * (inner / width))
+            inner = jnp.sum(weighted * r.scaled[0], axis=1, keepdims=True)
+            cotangent = inv_rms * (weighted - r.scaled[0] * (inner / width))
             if term == 0:
-                r.adjoint[...] = r.pieces[1, own_rows, :].astype(full) + cotangent
+                adjoint_out[...] = cotangent
             else:
-                r.adjoint[...] += cotangent
+                adjoint_out[...] += cotangent
             if not final:
                 r.pieces[2 + term, own_rows, :] = cotangent.astype(low)
 
-        out_copy = load(6, r.adjoint, adjoint_hbm)
-        out_copy.start()
-        near_sum(CHUNKS - 1)
         for item in range(1 + ITERS):
             gather_drain(item)
         for item in range(3 + ITERS):
-            for mask in order:
-                heads_copy(item, mask).wait_send()
+            heads_drain(item)
         for item in range(3 * ITERS):
-            for mask in order:
-                grads_copy(item, mask).wait_send()
-        for chunk in range(CHUNKS):
-            for term in range(ITERS):
-                for step in range(chips):
-                    hand_copy(term, step, chunk).wait_send()
-                    if step:
-                        far_copy(term, step, chunk).wait_send()
-            for step in range(1, tensor_count):
-                near_copy(step, chunk).wait_send()
-        for chunk in range(CHUNKS):
-            for mask in order:
-                wide_copy(mask, chunk).wait()
-        value = r.gain_mid[...]
+            grads_drain(item)
+        for term in range(ITERS):
+            reduce_drain(term)
+        block = r.gain_far.at[pl.ds(1, seq_count - 1)]
+        remote(
+            block, block, r.wide_send.at[0], r.wide_recv.at[0], "seq", flipped(me_seq, 1, bits)
+        ).wait()
+        value = r.gain_own[...]
         for mask in order:
             value = value + r.gain_far[mask]
-        r.gain_out[...] = value * length ** (-0.5)
-        out_copy.wait()
-        gain_copy = load(0, r.gain_out, gain_out_hbm)
-        gain_copy.start()
-        gain_copy.wait()
+        r.gain_mid[...] = value
+        for step in range(1, tensor_count):
+            near_copy(step).start()
+        block = r.gain_near.at[pl.ds(1, tensor_count - 1)]
+        remote(block, block, r.near_send.at[0], r.near_recv.at[0], "tensor", partner).wait()
+        for step in range(1, tensor_count):
+            value = value + r.gain_near[step]
+        gain_out[...] = value
 
     anywhere = pl.BlockSpec(memory_space=pl.ANY)
     adjoint, gain_grad = pl.pallas_call(
@@ -774,10 +810,10 @@
             jax.ShapeDtypeStruct((gain_rows, HEAD_DIM), full),
         ],
         in_specs=[anywhere] * 10,
-        out_specs=[anywhere] * 2,
+        out_specs=[pl.BlockSpec(memory_space=pltpu.VMEM)] * 2,
         scratch_shapes=list(scratch.values()),
         compiler_params=pltpu.CompilerParams(
-            collective_id=0, has_side_effects=True, vmem_limit_bytes=67043328
+            collective_id=0, has_side_effects=True, vmem_limit_bytes=62 << 20
         ),
     )(
         fixed_point,
@@ -791,7 +827,8 @@
         jnp.asarray(cosine),
         jnp.asarray(sine),
     )
-    return adjoint, gain_grad.reshape(width)
+    adjoint = incoming.astype(full) + adjoint
+    return adjoint, gain_grad.reshape(width) * length ** (-0.5)
 
 
 def solution(mesh):

time: 146 us -> 123 us (0.84)
  Pallas kernels: 142 us -> 118 us
  other arithmetic: 0 us -> 3.2 us
  local copies, waits for them, and re-layouts: 3.19 us -> 0.01 us
    pallas_call x1, Pallas kernels: 142 us -> 118 us  [fused_body(): pl.pallas_call(kernel, out_shape=[jax.ShapeDtypeStruct((rows, width), ful...]
    unnamed x2, local copies, waits for them, and re-layouts: 3.19 us -> 0.01 us
    add x0 -> x1, other arithmetic: none -> 1.88 us  [fused_body(): adjoint = incoming.astype(full) + adjoint]
where the time goes in v2:
time: 123 us; the launch traced here: 122 us
  Pallas kernels  118 us (96%)
  other arithmetic  3.2 us (3%)
    pallas_call x1, Pallas kernels, fused_body(): pl.pallas_call(kernel, out_shape=[jax.ShapeDtypeStruct((rows, width), ful...  118 us

profile of v2, /device:TPU:0, one launch (start us, length us, event | category | flops | bytes accessed | tf_op | source)
XLA Modules:
  0.0 122.3 jit_solution(12035531650713102451)
XLA Ops:
  0.6 0.0 copy-start
  0.6 118.4 %shard_map.113 = (f32[32,4096]{1,0:T(8,128)}, f32[32,128]{1,0:T(8,128)}) custom-call(bf16[32,4096]{1,0:T(8,128)(2,1)} %refs_0_.1, bf16[32,4096]{1,0:T(8,128)(2,1)} %refs_1_.1, f32[1,4096]{1,0:T(1,128)} %bitcast.3, bf16[4096,1024]{1,0:T(8,128)(2,1)} %refs_3_.1, bf16[4096,1024]{1,0:T(8,128)(2,1)} %refs_4_.1, bf16[4096,1024]{1,0:T(8,128)(2,1)} %refs_5_.1, ...), custom_call_target="tpu_custom_call" | custom-call | tf_op jit(solution)/shard_map/pallas_call | solution.py:806
  119.1 0.0 copy-done
  119.1 1.9 %convert_add_fusion = f32[32,4096]{1,0:T(8,128)} fusion(f32[32,4096]{1,0:T(8,128)} %get-tuple-element.4, bf16[32,4096]{1,0:T(8,128)(2,1)S(1)} %copy-done), kind=kLoop, calls=%fused_computation | loop fusion | flops 262144 | bytes 1310720 | tf_op jit(solution)/shard_map/add | solution.py:830
  121.0 1.3 %multiply_bitcast_fusion = f32[4096]{0:T(1024)} fusion(f32[32,128]{1,0:T(8,128)} %get-tuple-element.5), kind=kLoop, calls=%fused_computation.1 | loop fusion | flops 4096 | bytes 32768 | tf_op jit(solution)/shard_map/mul | solution.py:831
Async XLA Ops:
  0.6 118.4 %copy-start = (bf16[32,4096]{1,0:T(8,128)(2,1)S(1)}, bf16[32,4096]{1,0:T(8,128)(2,1)}, u32[]{:S(2)}) copy-start(bf16[32,4096]{1,0:T(8,128)(2,1)} %refs_1_.1) | copy-start | bytes 786436

commit v3 on v2

--- a/solution.py
+++ b/solution.py
@@ -180,6 +180,7 @@
 
 
 CHUNKS = 4
+HALVES = 2
 MESH = pl.DeviceIdType.MESH
 
 
@@ -222,6 +223,9 @@
     length = tokens * seq_count
     blocks = layout.shape[0]
     part = width // CHUNKS
+    lines = rows // HALVES
+    groups = length // rows
+    half_tokens = tensor_count * lines
     score_scale = HEAD_DIM ** (-0.5)
     gain_rows = width // HEAD_DIM
     gain_part = gain_rows // CHUNKS
@@ -230,32 +234,35 @@
     low, full = jnp.bfloat16, jnp.float32
     dma = pltpu.SemaphoreType.DMA
     scratch = {
-        "wq": pltpu.VMEM((width, head_width), low),
-        "wk": pltpu.VMEM((width, head_width), low),
-        "wv": pltpu.VMEM((width, head_width), low),
-        "wo": pltpu.VMEM((head_width, width), low),
-        "point": pltpu.VMEM((chips, rows, width), low),
+        "weights": pltpu.VMEM((4 * CHUNKS + 1, part, head_width), low),
+        "point": pltpu.VMEM((chips, HALVES, lines, width), low),
         "gain": pltpu.VMEM((1, width), full),
         "layout": pltpu.VMEM(layout.shape, jnp.int32),
         "cosine": pltpu.VMEM((length, HEAD_DIM), full),
         "sine": pltpu.VMEM((length, HEAD_DIM), full),
         "bias": pltpu.VMEM((blocks, length), full),
-        "scaled": pltpu.VMEM((chips, rows, width), full),
-        "pieces": pltpu.VMEM((1 + ITERS, tokens, width), low),
-        "acc": pltpu.VMEM((4, tokens, head_width), full),
-        "heads_out": pltpu.VMEM((3 + ITERS, seq_count, tokens, HEAD_DIM), low),
-        "heads_in": pltpu.VMEM((3 + ITERS, length, HEAD_DIM), low),
+        "scaled": pltpu.VMEM((chips, HALVES, lines, width), full),
+        "pieces": pltpu.VMEM((2, tokens, width), low),
+        "series": pltpu.VMEM((ITERS - 1, HALVES, tensor_count, lines, width), low),
+        "heads_out": pltpu.VMEM((4, seq_count, tokens, HEAD_DIM), low),
+        "heads_in": pltpu.VMEM((4, length, HEAD_DIM), low),
+        "late_out": pltpu.VMEM(
+            (ITERS - 1, HALVES, seq_count, tensor_count, lines, HEAD_DIM), low
+        ),
+        "late_in": pltpu.VMEM((ITERS - 1, groups, HALVES, lines, HEAD_DIM), low),
         "probs": pltpu.VMEM((length, length), low),
         "key_acc": pltpu.VMEM((length, HEAD_DIM), full),
         "probs_turned": pltpu.VMEM((length, length), low),
-        "grads_out": pltpu.VMEM((3 * ITERS, length, HEAD_DIM), low),
-        "grads_in": pltpu.VMEM((3 * ITERS, tokens, head_width), low),
-        "total": pltpu.VMEM((tokens, width), full),
-        "hand_out": pltpu.VMEM((ITERS * chips, rows, width), low),
-        "hand_in": pltpu.VMEM((ITERS * chips, rows, width), low),
-        "far_out": pltpu.VMEM((ITERS * chips, rows, width), low),
-        "far_in": pltpu.VMEM((ITERS * chips, rows, width), low),
-        "normed_grad": pltpu.VMEM((rows, width), full),
+        "grads_out": pltpu.VMEM((2 * ITERS, length, HEAD_DIM), low),
+        "grads_in": pltpu.VMEM((2 * ITERS, tokens, head_width), low),
+        "query_out": pltpu.VMEM((ITERS, groups, HALVES, lines, HEAD_DIM), low),
+        "query_in": pltpu.VMEM((ITERS, HALVES, tensor_count, lines, head_width), low),
+        "total": pltpu.VMEM((tensor_count, HALVES, lines, width), full),
+        "hand_out": pltpu.VMEM((ITERS, HALVES, chips, lines, width), low),
+        "hand_in": pltpu.VMEM((ITERS, HALVES, chips, lines, width), low),
+        "far_out": pltpu.VMEM((ITERS, HALVES, chips - 1, lines, width), low),
+        "far_in": pltpu.VMEM((ITERS, HALVES, chips - 1, lines, width), low),
+        "normed_grad": pltpu.VMEM((HALVES, lines, width), full),
         "gain_sum": pltpu.VMEM((1, width), full),
         "gain_own": pltpu.VMEM((gain_rows, HEAD_DIM), full),
         "gain_near": pltpu.VMEM((tensor_count, gain_rows, HEAD_DIM), full),
@@ -263,17 +270,24 @@
         "gain_far": pltpu.VMEM((seq_count, gain_rows, HEAD_DIM), full),
         "load_sem": dma((6,)),
         "weight_sem": dma((CHUNKS + 1,)),
-        "gather_send": dma((1 + ITERS,)),
-        "gather_far": dma((1 + ITERS, CHUNKS * (chips - 1))),
-        "gather_near": dma((1 + ITERS, CHUNKS)),
-        "heads_send": dma((3 + ITERS,)),
-        "heads_recv": dma((3 + ITERS,)),
-        "grads_send": dma((3 * ITERS,)),
-        "grads_recv": dma((3 * ITERS,)),
+        "gather_send": dma((2,)),
+        "gather_far": dma((2, CHUNKS * (chips - 1))),
+        "gather_near": dma((2, CHUNKS)),
+        "series_send": dma(((ITERS - 1) * HALVES,)),
+        "series_far": dma(((ITERS - 1) * HALVES, CHUNKS * (chips - 1))),
+        "series_near": dma(((ITERS - 1) * HALVES, CHUNKS)),
+        "heads_send": dma((4,)),
+        "heads_recv": dma((4,)),
+        "late_send": dma(((ITERS - 1) * HALVES,)),
+        "late_recv": dma(((ITERS - 1) * HALVES,)),
+        "grads_send": dma((2 * ITERS,)),
+        "grads_recv": dma((2 * ITERS,)),
+        "query_send": dma((ITERS * HALVES,)),
+        "query_recv": dma((ITERS * HALVES,)),
         "hand_send": dma((ITERS,)),
-        "hand_recv": dma((ITERS, CHUNKS)),
+        "hand_recv": dma((ITERS * HALVES, CHUNKS)),
         "far_send": dma((ITERS,)),
-        "far_recv": dma((ITERS, CHUNKS)),
+        "far_recv": dma((ITERS * HALVES, CHUNKS)),
         "point_send": dma((1,)),
         "point_recv": dma((1,)),
         "near_send": dma((1,)),
@@ -325,21 +339,32 @@
         for index in (0, 1, 2, 3):
             loads[index].start()
 
+        def block_of(item, chunk):
+            return item * CHUNKS + chunk
+
         def weight_load(item, chunk):
-            source = (wq_hbm, wk_hbm, wv_hbm)[item]
-            target = (r.wq, r.wk, r.wv)[item]
-            place = window(chunk, part)
+            if item == 3:
+                source = wo_hbm.at[:, window(chunk, part)]
+            else:
+                source = (wv_hbm, wk_hbm, wq_hbm)[item].at[chunk]
+            target = r.weights.at[1 + block_of(item, chunk)]
             return pltpu.make_async_copy(
-                source.at[place, :], target.at[place, :], r.weight_sem.at[chunk]
-            )
-
-        def weight_ready(chunk):
-            whole = pl.ds(0, 3 * part)
+                source, target, r.weight_sem.at[CHUNKS if item == 3 else chunk]
+            )
+
+        def weight_ready(index, count):
             pltpu.make_async_copy(
-                wq_hbm.at[whole, :], r.wq.at[whole, :], r.weight_sem.at[chunk]
+                wq_hbm.at[pl.ds(0, count)], r.weights.at[pl.ds(0, count)], r.weight_sem.at[index]
             ).wait()
 
-        out_load = pltpu.make_async_copy(wo_hbm, r.wo, r.weight_sem.at[CHUNKS])
+        def turn_weights(first, last):
+            def body(block, carry):
+                for line in range(0, part, HEAD_DIM):
+                    strip = slice(line, line + HEAD_DIM)
+                    r.weights[block, :, strip] = r.weights[block + 1, strip, :].T
+                return carry
+
+            lax.fori_loop(first * CHUNKS, last * CHUNKS, body, 0)
 
         def remote(source, target, send, recv, axis, peer):
             return pltpu.make_async_remote_copy(
@@ -351,21 +376,30 @@
                 device_id_type=MESH,
             )
 
-        def gather_copy(item, chunk, recv, origin, peer):
-            block = r.pieces.at[item, window(origin, rows), window(chunk, part)]
-            return remote(block, block, r.gather_send.at[item], recv, "tensor", peer)
+        def gather_parts(item, chunk, origin):
+            place = window(chunk, part)
+            if isinstance(item, tuple):
+                term, half = item
+                index = (term - 1) * HALVES + half
+                block = r.series.at[term - 1, half, origin, :, place]
+                return block, r.series_send.at[index], r.series_far, r.series_near, index
+            block = r.pieces.at[item, window(origin, rows), place]
+            return block, r.gather_send.at[item], r.gather_far, r.gather_near, item
 
         def gather_far(item, chunk, step):
+            block, send, far, near, index = gather_parts(item, chunk, me)
+            recv = far.at[index, chunk * (chips - 1) + step - 1]
             peer = 2 * lax.rem(chip + step, chips) + core
-            recv = r.gather_far.at[item, chunk * (chips - 1) + step - 1]
-            return gather_copy(item, chunk, recv, me, peer)
+            return remote(block, block, send, recv, "tensor", peer)
 
         def gather_near(item, chunk):
-            return gather_copy(item, chunk, r.gather_near.at[item, chunk], me, partner)
+            block, send, far, near, index = gather_parts(item, chunk, me)
+            return remote(block, block, send, near.at[index, chunk], "tensor", partner)
 
         def gather_pass(item, chunk, step):
             origin = 2 * lax.rem(chip + chips - step, chips) + core
-            return gather_copy(item, chunk, r.gather_near.at[item, chunk], origin, partner)
+            block, send, far, near, index = gather_parts(item, chunk, origin)
+            return remote(block, block, send, near.at[index, chunk], "tensor", partner)
 
         def gather_start(item):
             for chunk in range(CHUNKS):
@@ -379,16 +413,23 @@
                 gather_pass(item, chunk, step).start()
 
         def gather_ready(item, chunk):
-            block = r.pieces.at[item, pl.ds(0, chips * rows), window(chunk, part)]
-            send, recv = r.gather_send.at[item], r.gather_near.at[item, chunk]
-            remote(block, block, send, recv, "tensor", partner).wait_recv()
+            place = window(chunk, part)
+            block, send, far, near, index = gather_parts(item, chunk, 0)
+            if isinstance(item, tuple):
+                block = r.series.at[item[0] - 1, item[1], pl.ds(0, chips), :, place]
+            else:
+                block = r.pieces.at[item, pl.ds(0, chips * rows), place]
+            remote(block, block, send, near.at[index, chunk], "tensor", partner).wait_recv()
 
         def gather_drain(item):
-            block = r.pieces.at[item, pl.ds(0, (2 * chips - 1) * rows), :]
-            send, recv = r.gather_send.at[item], r.gather_near.at[item, 0]
-            remote(block, block, send, recv, "tensor", partner).wait_send()
-
-        def gather_each(item, use, after=None):
+            block, send, far, near, index = gather_parts(item, 0, 0)
+            if isinstance(item, tuple):
+                block = r.series.at[item[0] - 1, item[1], pl.ds(0, 2 * chips - 1)]
+            else:
+                block = r.pieces.at[item, pl.ds(0, (2 * chips - 1) * rows), :]
+            remote(block, block, send, near.at[index, 0], "tensor", partner).wait_send()
+
+        def gather_each(item, use, after=None, count=CHUNKS):
             gather_relay(item, 0)
 
             def body(chunk, carry):
@@ -406,7 +447,10 @@
                 use(chunk)
                 return carry
 
-            lax.fori_loop(0, CHUNKS, body, 0)
+            lax.fori_loop(0, count, body, 0)
+
+        def columns_of(slot):
+            return slice(slot * head_width, (slot + 1) * head_width)
 
         def point_copy(step):
             return remote(
@@ -428,10 +472,11 @@
                 flipped(me_seq, mask, bits),
             )
 
-        def heads_start(item, slot, turn):
+        def heads_start(item, turn):
             for mask in order + [0]:
-                columns = window(flipped(me_seq, mask, bits), HEAD_DIM)
-                values = r.acc[slot, :, columns]
+                peer = flipped(me_seq, mask, bits)
+                columns = window(item * seq_count + peer, HEAD_DIM)
+                values = r.total[:, :, :, columns].reshape(tokens, HEAD_DIM)
                 if turn:
                     values = (
                         values * r.cosine[own_tokens, :]
@@ -444,6 +489,34 @@
             for mask in order:
                 heads_copy(item, mask).start()
 
+        def late_copy(term, half, mask):
+            index = (term - 1) * HALVES + half
+            return remote(
+                r.late_out.at[term - 1, half, mask],
+                r.late_in.at[term - 1, window(me_seq, tensor_count), half],
+                r.late_send.at[index],
+                r.late_recv.at[index],
+                "seq",
+                flipped(me_seq, mask, bits),
+            )
+
+        def late_start(term, half):
+            for mask in order + [0]:
+                columns = window(flipped(me_seq, mask, bits), HEAD_DIM)
+                values = r.total[:, half, :, columns].astype(low)
+                if mask:
+                    r.late_out[term - 1, half, mask] = values
+                else:
+                    r.late_in[term - 1, window(me_seq, tensor_count), half] = values
+            for mask in order:
+                late_copy(term, half, mask).start()
+
+        def late_whole(term, half):
+            block = r.late_out.at[term - 1, half, pl.ds(1, seq_count - 1)]
+            index = (term - 1) * HALVES + half
+            send, recv = r.late_send.at[index], r.late_recv.at[index]
+            return remote(block, block, send, recv, "seq", flipped(me_seq, 1, bits))
+
         def heads_ready(item):
             block = r.heads_in.at[item, pl.ds(0, (seq_count - 1) * tokens), :]
             send, recv = r.heads_send.at[item], r.heads_recv.at[item]
@@ -480,46 +553,64 @@
             send, recv = r.grads_send.at[item], r.grads_recv.at[item]
             remote(block, block, send, recv, "seq", flipped(me_seq, 1, bits)).wait_send()
 
-        def hand_copy(term, step, chunk):
+        def query_copy(term, half, mask):
+            peer = flipped(me_seq, mask, bits)
+            index = term * HALVES + half
+            return remote(
+                r.query_out.at[term, window(peer, tensor_count), half],
+                r.query_in.at[term, half, :, :, own_columns],
+                r.query_send.at[index],
+                r.query_recv.at[index],
+                "seq",
+                peer,
+            )
+
+        def query_start(term):
+            for half in range(HALVES):
+                for mask in order:
+                    query_copy(term, half, mask).start()
+                own = r.query_out[term, window(me_seq, tensor_count), half]
+                r.query_in[term, half, :, :, own_columns] = own
+
+        def query_whole(term, half):
+            block = r.query_in.at[term, half, :, :, pl.ds(0, (seq_count - 1) * HEAD_DIM)]
+            index = term * HALVES + half
+            send, recv = r.query_send.at[index], r.query_recv.at[index]
+            return remote(block, block, send, recv, "seq", flipped(me_seq, 1, bits))
+
+        def hand_copy(term, half, chunk):
             place = window(chunk, part)
-            item = term * chips + step
             return remote(
-                r.hand_out.at[item, :, place],
-                r.hand_in.at[item, :, place],
+                r.hand_out.at[term, half, :, :, place],
+                r.hand_in.at[term, half, :, :, place],
                 r.hand_send.at[term],
-                r.hand_recv.at[term, chunk],
+                r.hand_recv.at[term * HALVES + half, chunk],
                 "tensor",
                 partner,
             )
 
-        def far_copy(term, step, chunk):
+        def far_copy(term, half, step, chunk):
             place = window(chunk, part)
-            item = term * chips + step
             return remote(
-                r.far_out.at[item, :, place],
-                r.far_in.at[item, :, place],
+                r.far_out.at[term, half, step - 1, :, place],
+                r.far_in.at[term, half, step - 1, :, place],
                 r.far_send.at[term],
-                r.far_recv.at[term, chunk],
+                r.far_recv.at[term * HALVES + half, chunk],
                 "tensor",
                 2 * lax.rem(chip + step, chips) + core,
             )
 
-        def hand_ready(term, chunk):
-            block = r.hand_in.at[pl.ds(term * chips, chips), :, window(chunk, part)]
-            send, recv = r.hand_send.at[term], r.hand_recv.at[term, chunk]
+        def far_ready(term, half, chunk):
+            block = r.far_in.at[term, half, :, :, window(chunk, part)]
+            send, recv = r.far_send.at[term], r.far_recv.at[term * HALVES + half, chunk]
             remote(block, block, send, recv, "tensor", partner).wait_recv()
 
-        def far_ready(term, chunk):
-            block = r.far_in.at[pl.ds(term * chips + 1, chips - 1), :, window(chunk, part)]
-            send, recv = r.far_send.at[term], r.far_recv.at[term, chunk]
-            remote(block, block, send, recv, "tensor", partner).wait_recv()
-
         def reduce_drain(term):
-            block = r.hand_out.at[pl.ds(term * chips, chips)]
-            send, recv = r.hand_send.at[term], r.hand_recv.at[term, 0]
+            block = r.hand_out.at[term]
+            send, recv = r.hand_send.at[term], r.hand_recv.at[term * HALVES, 0]
             remote(block, block, send, recv, "tensor", partner).wait_send()
-            block = r.far_out.at[pl.ds(term * chips + 1, chips - 1)]
-            send, recv = r.far_send.at[term], r.far_recv.at[term, 0]
+            block = r.far_out.at[term]
+            send, recv = r.far_send.at[term], r.far_recv.at[term * HALVES, 0]
             remote(block, block, send, recv, "tensor", partner).wait_send()
 
         def wide_copy(mask, chunk):
@@ -548,18 +639,20 @@
         for chunk in range(CHUNKS):
             for item in range(3):
                 weight_load(item, chunk).start()
-        out_load.start()
+        for chunk in range(CHUNKS):
+            weight_load(3, chunk).start()
         for copy in loads[4:]:
             copy.start()
 
         def scale(step):
             point = r.point[step].astype(full)
-            inv_rms = lax.rsqrt(jnp.mean(point * point, axis=1, keepdims=True) + EPS)
+            inv_rms = lax.rsqrt(jnp.mean(point * point, axis=-1, keepdims=True) + EPS)
             r.scaled[step] = point * inv_rms
             return inv_rms
 
         inv_rms = scale(0)
-        r.pieces[0, own_rows, :] = (r.gain[...] * r.scaled[0]).astype(low)
+        normed = r.gain[...].reshape(1, 1, width) * r.scaled[0]
+        r.pieces[0, own_rows, :] = normed.astype(low).reshape(rows, width)
         pl.semaphore_wait(barrier, tensor_count - 1 + seq_count - 1)
         gather_start(0)
 
@@ -579,33 +672,50 @@
             < lax.broadcasted_iota(jnp.int32, (blocks, length), 0)
         )
         r.bias[...] = jnp.where(earlier & (chosen > 0.5), 0.0, MASKED)
-        r.acc[...] = jnp.zeros(r.acc.shape, full)
+        r.total[...] = jnp.zeros(r.total.shape, full)
+        spread_rows = (tensor_count, HALVES, lines, head_width)
+
+        def project_one(item, chunk):
+            place = window(chunk, part)
+            weight = r.weights[1 + block_of(2 - item, chunk)]
+            value = product(r.pieces[0, :, place], weight, 1, 0)
+            r.total[:, :, :, columns_of(item)] += value.reshape(spread_rows)
 
         def project(chunk):
+            weight_ready(chunk, 3)
+            for item in range(3):
+                project_one(item, chunk)
+
+        gather_each(0, project, lambda: gather_start(1), CHUNKS - 1)
+        for copy in loads[4:]:
+            copy.wait()
+        gather_ready(0, CHUNKS - 1)
+        weight_ready(CHUNKS - 1, 3)
+        for item in range(3):
+            project_one(item, CHUNKS - 1)
+            heads_start(item, item < 2)
+        weight_ready(CHUNKS, CHUNKS)
+
+        def pull_first(chunk):
             place = window(chunk, part)
-            weight_ready(chunk)
-            for item, weight in enumerate((r.wq, r.wk, r.wv)):
-                r.acc[item] += product(r.pieces[0, :, place], weight[place, :], 1, 0)
-
-        gather_each(0, project, lambda: gather_start(1))
-        loads[4].wait()
-        loads[5].wait()
-        heads_start(0, 0, True)
-        heads_start(1, 1, True)
-        heads_start(2, 2, False)
-
-        def pull(item):
+            weight = r.weights[1 + block_of(3, chunk)]
+            value = product(r.pieces[1, :, place], weight, 1, 1)
+            r.total[:, :, :, columns_of(3)] += value.reshape(spread_rows)
+
+        gather_each(1, pull_first)
+        heads_start(3, False)
+
+        def pull(term, half):
             def use(chunk):
                 place = window(chunk, part)
-                r.acc[3] += product(r.pieces[item, :, place], r.wo[:, place], 1, 1)
+                piece = r.series[term - 1, half, :, :, place].reshape(half_tokens, part)
+                value = product(piece, r.weights[block_of(3, chunk)], 1, 0)
+                r.total[:, half, :, :head_width] += value.reshape(tensor_count, lines, head_width)
 
             return use
-
-        out_load.wait()
-        gather_each(1, pull(1))
-        heads_start(3, 3, False)
         for step in range(1, chips):
             point_copy(step).start()
+        turn_weights(0, 3)
 
         block = r.point.at[pl.ds(1, chips - 1)]
         remote(block, block, r.point_send.at[0], r.point_recv.at[0], "tensor", partner).wait()
@@ -645,12 +755,19 @@
 
         for base in range(0, seq_count, group):
             forward(base)
+        turn_weights(3, 4)
 
         def turned_back(values, place):
             return (
                 values * r.cosine[place, :]
                 - pltpu.roll(values, HEAD_DIM // 2, 1) * r.sine[place, :]
             ).astype(low)
+
+        def grad_rows(term, first, count):
+            if term == 0:
+                return r.heads_in[3, pl.ds(first * tokens, count * tokens), :]
+            block = r.late_in[term - 1, pl.ds(first * tensor_count, count * tensor_count)]
+            return block.reshape(count * tokens, HEAD_DIM)
 
         def backward(term):
             r.key_acc[...] = jnp.zeros(r.key_acc.shape, full)
@@ -658,24 +775,30 @@
                 later = slice(base * tokens, length)
                 for step in range(group):
                     place = slice((base + step) * tokens, (base + step + 1) * tokens)
-                    r.grads_out[3 * term + 2, place, :] = product(
-                        r.probs_turned[place, later], r.heads_in[3 + term, later, :], 1, 0
+                    r.grads_out[2 * term + 1, place, :] = product(
+                        r.probs_turned[place, later],
+                        grad_rows(term, base, seq_count - base),
+                        1,
+                        0,
                     ).astype(low)
-            grads_start(3 * term + 2)
+            grads_start(2 * term + 1)
 
             def at(base):
                 span = (base + group) * tokens
 
                 def body(step, carry):
-                    place = window(base + group - 1 - step, tokens)
+                    at_block = base + group - 1 - step
+                    place = window(at_block, tokens)
                     probs = r.probs[place, :span]
-                    grad_low = r.heads_in[3 + term, place, :]
+                    grad_low = grad_rows(term, at_block, 1)
                     grad_probs = product(grad_low, r.heads_in[2, :span, :], 1, 1)
                     wide = probs.astype(full)
                     delta = jnp.sum(wide * grad_probs, axis=1, keepdims=True)
                     grad_scores = (wide * (grad_probs - delta)).astype(low)
                     grad_query = product(grad_scores, r.heads_in[1, :span, :], 1, 0) * score_scale
-                    r.grads_out[3 * term, place, :] = turned_back(grad_query, place)
+                    r.query_out[term, window(at_block, tensor_count)] = turned_back(
+                        grad_query, place
+                    ).reshape(tensor_count, HALVES, lines, HEAD_DIM)
                     r.key_acc[:span, :] += product(grad_scores, r.heads_in[0, place, :], 0, 0)
                     return carry
 
@@ -683,28 +806,27 @@
 
             for base in reversed(range(0, seq_count, group)):
                 at(base)
-            r.grads_out[3 * term + 1] = turned_back(r.key_acc[...] * score_scale, slice(None))
-            grads_start(3 * term + 1)
-            grads_start(3 * term)
-
-        def hand_on(term, chunk):
+            r.grads_out[2 * term] = turned_back(r.key_acc[...] * score_scale, slice(None))
+            grads_start(2 * term)
+            query_start(term)
+
+        def hand_on(term, half, chunk):
             place = window(chunk, part)
-            hand_ready(term, chunk)
+            hand_copy(term, half, chunk).wait_recv()
             gain_term = jnp.zeros((1, part), full)
             for step in range(chips):
                 owner = 2 * lax.rem(chip + step, chips) + core
-                pair = r.total[window(owner, rows), place] + r.hand_in[
-                    term * chips + step, :, place
-                ].astype(full)
+                handed = r.hand_in[term, half, step, :, place].astype(full)
+                pair = r.total[owner, half, :, place] + handed
                 if step:
-                    r.far_out[term * chips + step, :, place] = pair.astype(low)
-                    far_copy(term, step, chunk).start()
+                    r.far_out[term, half, step - 1, :, place] = pair.astype(low)
+                    far_copy(term, half, step, chunk).start()
                 else:
-                    r.normed_grad[:, place] = pair
-                gain_term += jnp.sum(pair * r.scaled[step, :, place], axis=0, keepdims=True)
-            if term:
+                    r.normed_grad[half, :, place] = pair
+                gain_term += jnp.sum(pair * r.scaled[step, half, :, place], axis=0, keepdims=True)
+            if term + half:
                 gain_term += r.gain_sum[:, place]
-            if term < ITERS - 1:
+            if term < ITERS - 1 or half < HALVES - 1:
                 r.gain_sum[:, place] = gain_term
                 return
             r.gain_own[window(chunk, gain_part), :] = jnp.concatenate(
@@ -715,75 +837,98 @@
                 wide_copy(mask, chunk).start()
 
         def push(term):
-            for item, weight in ((2, r.wv), (1, r.wk)):
-                grads_ready(3 * term + item)
+            for item in (1, 0):
+                grads_ready(2 * term + item)
 
                 def body(chunk, carry):
                     place = window(chunk, part)
-                    value = product(r.grads_in[3 * term + item], weight[place, :], 1, 1)
-                    if item == 1:
-                        value = value + r.total[:, place]
-                    r.total[:, place] = value
+                    weight = r.weights[block_of(1 - item, chunk)]
+                    value = product(r.grads_in[2 * term + item], weight, 1, 0)
+                    value = value.reshape(tensor_count, HALVES, lines, part)
+                    if item == 0:
+                        value = value + r.total[:, :, :, place]
+                    r.total[:, :, :, place] = value
                     return carry
 
                 lax.fori_loop(0, CHUNKS, body, 0)
-            grads_ready(3 * term)
-
-            def last(chunk, carry):
-                place = window(chunk, part)
-                r.total[:, place] += product(r.grads_in[3 * term], r.wq[place, :], 1, 1)
-                for step in range(chips):
-                    other = 2 * lax.rem(chip + step, chips) + 1 - core
-                    r.hand_out[term * chips + step, :, place] = r.total[
-                        window(other, rows), place
-                    ].astype(low)
-                for step in range(chips):
-                    hand_copy(term, step, chunk).start()
-
-                @pl.when(chunk > 0)
-                def _():
-                    hand_on(term, chunk - 1)
-
-                return carry
-
-            lax.fori_loop(0, CHUNKS, last, 0)
-            hand_on(term, CHUNKS - 1)
+            for half in range(HALVES):
+                query_whole(term, half).wait_recv()
+
+                def last(chunk, carry):
+                    place = window(chunk, part)
+                    grads = r.query_in[term, half].reshape(half_tokens, head_width)
+                    value = product(grads, r.weights[block_of(2, chunk)], 1, 0)
+                    r.total[:, half, :, place] += value.reshape(tensor_count, lines, part)
+                    for step in range(chips):
+                        other = 2 * lax.rem(chip + step, chips) + 1 - core
+                        r.hand_out[term, half, step, :, place] = r.total[
+                            other, half, :, place
+                        ].astype(low)
+                    hand_copy(term, half, chunk).start()
+
+                    @pl.when(chunk > 0)
+                    def _():
+                        hand_on(term, half, chunk - 1)
+
+                    if half:
+
+                        @pl.when(chunk == 0)
+                        def _():
+                            hand_on(term, half - 1, CHUNKS - 1)
+
+                    return carry
+
+                lax.fori_loop(0, CHUNKS, last, 0)
+            hand_on(term, HALVES - 1, CHUNKS - 1)
+
+        def finish(term, half):
+            for chunk in range(CHUNKS):
+                place = slice(chunk * part, (chunk + 1) * part)
+                far_ready(term, half, chunk)
+                value = r.normed_grad[half, :, place]
+                for step in range(1, chips):
+                    value = value + r.far_in[term, half, step - 1, :, place].astype(full)
+                r.normed_grad[half, :, place] = value
+            scaled = r.scaled[0, half]
+            weighted = r.gain[...] * r.normed_grad[half]
+            inner = jnp.sum(weighted * scaled, axis=1, keepdims=True)
+            cotangent = inv_rms[half] * (weighted - scaled * (inner / width))
+            if term == 0:
+                adjoint_out[half] = cotangent
+            else:
+                adjoint_out[half] += cotangent
+            if term < ITERS - 1:
+                r.series[term, half, me] = cotangent.astype(low)
+                gather_start((term + 1, half))
 
         for term in range(ITERS):
             if term:
-                r.acc[3] = jnp.zeros((tokens, head_width), full)
-                gather_start(1 + term)
-                gather_each(1 + term, pull(1 + term))
-                heads_start(3 + term, 3, False)
+                r.total[:, :, :, :head_width] = jnp.zeros(spread_rows, full)
+                for half in range(HALVES):
+                    gather_each((term, half), pull(term, half))
+                    late_start(term, half)
+                for half in range(HALVES):
+                    late_whole(term, half).wait_recv()
             else:
                 heads_ready(2)
-            heads_ready(3 + term)
+                heads_ready(3)
             backward(term)
             push(term)
-            final = term == ITERS - 1
-            for chunk in range(CHUNKS):
-                place = slice(chunk * part, (chunk + 1) * part)
-                value = r.normed_grad[:, place]
-                far_ready(term, chunk)
-                for step in range(1, chips):
-                    value = value + r.far_in[term * chips + step, :, place].astype(full)
-                r.normed_grad[:, place] = value
-            weighted = r.gain[...] * r.normed_grad[...]
-            inner = jnp.sum(weighted * r.scaled[0], axis=1, keepdims=True)
-            cotangent = inv_rms * (weighted - r.scaled[0] * (inner / width))
-            if term == 0:
-                adjoint_out[...] = cotangent
-            else:
-                adjoint_out[...] += cotangent
-            if not final:
-                r.pieces[2 + term, own_rows, :] = cotangent.astype(low)
-
-        for item in range(1 + ITERS):
+            for half in range(HALVES):
+                finish(term, half)
+
+        for item in range(2):
             gather_drain(item)
-        for item in range(3 + ITERS):
+        for item in range(4):
             heads_drain(item)
-        for item in range(3 * ITERS):
+        for item in range(2 * ITERS):
             grads_drain(item)
+        for term in range(ITERS):
+            for half in range(HALVES):
+                query_whole(term, half).wait_send()
+                if term:
+                    gather_drain((term, half))
+                    late_whole(term, half).wait_send()
         for term in range(ITERS):
             reduce_drain(term)
         block = r.gain_far.at[pl.ds(1, seq_count - 1)]
@@ -806,28 +951,28 @@
     adjoint, gain_grad = pl.pallas_call(
         kernel,
         out_shape=[
-            jax.ShapeDtypeStruct((rows, width), full),
+            jax.ShapeDtypeStruct((HALVES, lines, width), full),
             jax.ShapeDtypeStruct((gain_rows, HEAD_DIM), full),
         ],
         in_specs=[anywhere] * 10,
         out_specs=[pl.BlockSpec(memory_space=pltpu.VMEM)] * 2,
         scratch_shapes=list(scratch.values()),
         compiler_params=pltpu.CompilerParams(
-            collective_id=0, has_side_effects=True, vmem_limit_bytes=62 << 20
+            collective_id=0, has_side_effects=True, vmem_limit_bytes=58 << 20
         ),
     )(
-        fixed_point,
+        fixed_point.reshape(HALVES, lines, width),
         incoming,
         norm_gain.reshape(1, width),
-        query_weight,
-        key_weight,
-        value_weight,
+        query_weight.reshape(CHUNKS, part, head_width),
+        key_weight.reshape(CHUNKS, part, head_width),
+        value_weight.reshape(CHUNKS, part, head_width),
         out_weight,
         layout,
         jnp.asarray(cosine),
         jnp.asarray(sine),
     )
-    adjoint = incoming.astype(full) + adjoint
+    adjoint = incoming.astype(full) + adjoint.reshape(rows, width)
     return adjoint, gain_grad.reshape(width) * length ** (-0.5)
 
 
@@ -850,11 +995,13 @@
         tokens = arrays[0].shape[0] * tensor
         fits = (
             tensor % 2 == 0
+            and tensor >= 4
             and seq & (seq - 1) == 0
             and heads == seq * tensor
             and tokens % 128 == 0
-            and arrays[0].shape[0] % 16 == 0
-            and arrays[0].shape[1] % (8 * HEAD_DIM * CHUNKS) == 0
+            and arrays[0].shape[0] % (16 * HALVES) == 0
+            and arrays[0].shape[1] == CHUNKS * arrays[3].shape[1]
+            and arrays[3].shape[1] % (8 * HEAD_DIM) == 0
         )
         return (fused_body if fits else ring_body)(*arrays)
 

time: 123 us -> 118 us (0.959)
  Pallas kernels: 118 us -> 113 us
    pallas_call x1, Pallas kernels: 118 us -> 113 us  [fused_body(): pl.pallas_call(kernel, out_shape=[jax.ShapeDtypeStruct((HALVES, lines, wi...]
where the time goes in v3:
time: 118 us; the launch traced here: 117 us
  Pallas kernels  113 us (96%)
  other arithmetic  3.2 us (3%)
    pallas_call x1, Pallas kernels, fused_body(): pl.pallas_call(kernel, out_shape=[jax.ShapeDtypeStruct((HALVES, lines, wi...  113 us

profile of v3, /device:TPU:0, one launch (start us, length us, event | category | flops | bytes accessed | tf_op | source)
XLA Modules:
  0.0 117.3 jit_solution(5800056300412610811)
XLA Ops:
  0.6 0.0 copy-start
  0.6 113.4 %shard_map.113 = (f32[2,16,4096]{2,1,0:T(8,128)}, f32[32,128]{1,0:T(8,128)}) custom-call(bf16[2,16,4096]{2,1,0:T(8,128)(2,1)} %bitcast.12, bf16[32,4096]{1,0:T(8,128)(2,1)} %refs_1_.1, f32[1,4096]{1,0:T(1,128)} %bitcast.13, bf16[4,1024,1024]{2,1,0:T(8,128)(2,1)} %bitcast.9, bf16[4,1024,1024]{2,1,0:T(8,128)(2,1)} %bitcast.10, ...), custom_call_target="tpu_custom_call" | custom-call | tf_op jit(solution)/shard_map/pallas_call | solution.py:951
  114.0 0.0 copy-done
  114.1 1.9 %bitcast_add_fusion = f32[32,4096]{1,0:T(8,128)} fusion(f32[2,16,4096]{2,1,0:T(8,128)} %get-tuple-element.4, bf16[32,4096]{1,0:T(8,128)(2,1)S(1)} %copy-done), kind=kLoop, calls=%fused_computation | loop fusion | flops 262144 | bytes 1310720 | tf_op jit(solution)/shard_map/add | solution.py:975
  115.9 1.3 %multiply_bitcast_fusion = f32[4096]{0:T(1024)} fusion(f32[32,128]{1,0:T(8,128)} %get-tuple-element.5), kind=kLoop, calls=%fused_computation.1 | loop fusion | flops 4096 | bytes 32768 | tf_op jit(solution)/shard_map/mul | solution.py:976
Async XLA Ops:
  0.6 113.4 %copy-start = (bf16[32,4096]{1,0:T(8,128)(2,1)S(1)}, bf16[32,4096]{1,0:T(8,128)(2,1)}, u32[]{:S(2)}) copy-start(bf16[32,4096]{1,0:T(8,128)(2,1)} %refs_1_.1) | copy-start | bytes 786436

commit v4 on v3

--- a/solution.py
+++ b/solution.py
@@ -181,6 +181,7 @@
 
 CHUNKS = 4
 HALVES = 2
+LAG = 2
 MESH = pl.DeviceIdType.MESH
 
 
@@ -235,14 +236,14 @@
     dma = pltpu.SemaphoreType.DMA
     scratch = {
         "weights": pltpu.VMEM((4 * CHUNKS + 1, part, head_width), low),
-        "point": pltpu.VMEM((chips, HALVES, lines, width), low),
+        "inverse": pltpu.VMEM((tokens, HEAD_DIM), full),
         "gain": pltpu.VMEM((1, width), full),
         "layout": pltpu.VMEM(layout.shape, jnp.int32),
         "cosine": pltpu.VMEM((length, HEAD_DIM), full),
         "sine": pltpu.VMEM((length, HEAD_DIM), full),
         "bias": pltpu.VMEM((blocks, length), full),
-        "scaled": pltpu.VMEM((chips, HALVES, lines, width), full),
-        "pieces": pltpu.VMEM((2, tokens, width), low),
+        "scaled": pltpu.VMEM((HALVES, lines, width), full),
+        "pieces": pltpu.VMEM((3, tokens, width), low),
         "series": pltpu.VMEM((ITERS - 1, HALVES, tensor_count, lines, width), low),
         "heads_out": pltpu.VMEM((4, seq_count, tokens, HEAD_DIM), low),
         "heads_in": pltpu.VMEM((4, length, HEAD_DIM), low),
@@ -270,9 +271,9 @@
         "gain_far": pltpu.VMEM((seq_count, gain_rows, HEAD_DIM), full),
         "load_sem": dma((6,)),
         "weight_sem": dma((CHUNKS + 1,)),
-        "gather_send": dma((2,)),
-        "gather_far": dma((2, CHUNKS * (chips - 1))),
-        "gather_near": dma((2, CHUNKS)),
+        "gather_send": dma((3,)),
+        "gather_far": dma((3, CHUNKS * (chips - 1))),
+        "gather_near": dma((3, CHUNKS)),
         "series_send": dma(((ITERS - 1) * HALVES,)),
         "series_far": dma(((ITERS - 1) * HALVES, CHUNKS * (chips - 1))),
         "series_near": dma(((ITERS - 1) * HALVES, CHUNKS)),
@@ -288,8 +289,6 @@
         "hand_recv": dma((ITERS * HALVES, CHUNKS)),
         "far_send": dma((ITERS,)),
         "far_recv": dma((ITERS * HALVES, CHUNKS)),
-        "point_send": dma((1,)),
-        "point_recv": dma((1,)),
         "near_send": dma((1,)),
         "near_recv": dma((1,)),
         "wide_send": dma((1,)),
@@ -329,7 +328,7 @@
             return pltpu.make_async_copy(source, target, r.load_sem.at[index])
 
         loads = [
-            load(0, point_hbm, r.point.at[0]),
+            load(0, point_hbm, r.pieces.at[2, own_rows, :]),
             load(1, gain_hbm, r.gain),
             load(2, incoming_hbm, r.pieces.at[1, own_rows, :]),
             load(3, layout_hbm, r.layout),
@@ -451,16 +450,6 @@
 
         def columns_of(slot):
             return slice(slot * head_width, (slot + 1) * head_width)
-
-        def point_copy(step):
-            return remote(
-                r.point.at[0],
-                r.point.at[chips - step],
-                r.point_send.at[0],
-                r.point_recv.at[0],
-                "tensor",
-                2 * lax.rem(chip + step, chips) + core,
-            )
 
         def heads_copy(item, mask):
             return remote(
@@ -644,14 +633,10 @@
         for copy in loads[4:]:
             copy.start()
 
-        def scale(step):
-            point = r.point[step].astype(full)
-            inv_rms = lax.rsqrt(jnp.mean(point * point, axis=-1, keepdims=True) + EPS)
-            r.scaled[step] = point * inv_rms
-            return inv_rms
-
-        inv_rms = scale(0)
-        normed = r.gain[...].reshape(1, 1, width) * r.scaled[0]
+        point = r.pieces[2, own_rows, :].astype(full).reshape(HALVES, lines, width)
+        inv_rms = lax.rsqrt(jnp.mean(point * point, axis=-1, keepdims=True) + EPS)
+        r.scaled[...] = point * inv_rms
+        normed = r.gain[...].reshape(1, 1, width) * r.scaled[...]
         r.pieces[0, own_rows, :] = normed.astype(low).reshape(rows, width)
         pl.semaphore_wait(barrier, tensor_count - 1 + seq_count - 1)
         gather_start(0)
@@ -713,14 +698,13 @@
                 r.total[:, half, :, :head_width] += value.reshape(tensor_count, lines, head_width)
 
             return use
-        for step in range(1, chips):
-            point_copy(step).start()
+        gather_start(2)
         turn_weights(0, 3)
 
-        block = r.point.at[pl.ds(1, chips - 1)]
-        remote(block, block, r.point_send.at[0], r.point_recv.at[0], "tensor", partner).wait()
-        for step in range(1, chips):
-            scale(step)
+        for chunk in range(CHUNKS):
+            gather_relay(2, chunk)
+        for chunk in range(CHUNKS):
+            gather_ready(2, chunk)
 
         group = 2 if seq_count % 2 == 0 else 1
         heads_ready(0)
@@ -755,7 +739,6 @@
 
         for base in range(0, seq_count, group):
             forward(base)
-        turn_weights(3, 4)
 
         def turned_back(values, place):
             return (
@@ -810,20 +793,29 @@
             grads_start(2 * term)
             query_start(term)
 
-        def hand_on(term, half, chunk):
+        def hand_work(term, half, chunk):
             place = window(chunk, part)
-            hand_copy(term, half, chunk).wait_recv()
-            gain_term = jnp.zeros((1, part), full)
             for step in range(chips):
                 owner = 2 * lax.rem(chip + step, chips) + core
                 handed = r.hand_in[term, half, step, :, place].astype(full)
                 pair = r.total[owner, half, :, place] + handed
                 if step:
                     r.far_out[term, half, step - 1, :, place] = pair.astype(low)
-                    far_copy(term, half, step, chunk).start()
                 else:
                     r.normed_grad[half, :, place] = pair
-                gain_term += jnp.sum(pair * r.scaled[step, half, :, place], axis=0, keepdims=True)
+
+        def far_start(term, half, chunk):
+            for step in range(1, chips):
+                far_copy(term, half, step, chunk).start()
+
+        def gain_on(term, half, chunk):
+            place = window(chunk, part)
+            gain_term = jnp.zeros((lines, part), full)
+            for owner in range(tensor_count):
+                own = slice(owner * rows + half * lines, owner * rows + (half + 1) * lines)
+                scaled = r.pieces[2, own, place].astype(full) * r.inverse[own, :1]
+                gain_term += r.total[owner, half, :, place] * scaled
+            gain_term = jnp.sum(gain_term, axis=0, keepdims=True)
             if term + half:
                 gain_term += r.gain_sum[:, place]
             if term < ITERS - 1 or half < HALVES - 1:
@@ -833,11 +825,19 @@
                 [gain_term[:, line * HEAD_DIM : (line + 1) * HEAD_DIM] for line in range(gain_part)],
                 axis=0,
             )
-            for mask in order:
-                wide_copy(mask, chunk).start()
+        def invert():
+            for owner in range(tensor_count):
+                place = slice(owner * rows, (owner + 1) * rows)
+                point = r.pieces[2, place, :].astype(full)
+                inverse = lax.rsqrt(jnp.mean(point * point, axis=1, keepdims=True) + EPS)
+                r.inverse[place, :] = jnp.broadcast_to(inverse, (rows, HEAD_DIM))
 
         def push(term):
+            if term == 0:
+                invert()
             for item in (1, 0):
+                if term == 0 and item == 0:
+                    turn_weights(3, 4)
                 grads_ready(2 * term + item)
 
                 def body(chunk, carry):
@@ -851,35 +851,44 @@
                     return carry
 
                 lax.fori_loop(0, CHUNKS, body, 0)
+
+            def matmul(half, chunk):
+                place = window(chunk, part)
+                grads = r.query_in[term, half].reshape(half_tokens, head_width)
+                value = product(grads, r.weights[block_of(2, chunk)], 1, 0)
+                r.total[:, half, :, place] += value.reshape(tensor_count, lines, part)
+                for step in range(chips):
+                    other = 2 * lax.rem(chip + step, chips) + 1 - core
+                    r.hand_out[term, half, step, :, place] = r.total[
+                        other, half, :, place
+                    ].astype(low)
+                gain_on(term, half, chunk)
+
+            def stage(half, first, last, behind):
+                def body(chunk, carry):
+                    if behind is not None:
+                        earlier_half, shift = behind
+                        hand_copy(term, earlier_half, chunk + shift).wait_recv()
+                        hand_work(term, earlier_half, chunk + shift)
+                        if term < ITERS - 1:
+                            far_start(term, earlier_half, chunk + shift)
+                    if half is not None:
+                        matmul(half, chunk)
+                        hand_copy(term, half, chunk).start()
+                        if term == ITERS - 1 and half == HALVES - 1:
+                            for mask in order:
+                                wide_copy(mask, chunk).start()
+                    if behind is not None and term == ITERS - 1:
+                        far_start(term, earlier_half, chunk + shift)
+                    return carry
+
+                lax.fori_loop(first, last, body, 0)
+
             for half in range(HALVES):
                 query_whole(term, half).wait_recv()
-
-                def last(chunk, carry):
-                    place = window(chunk, part)
-                    grads = r.query_in[term, half].reshape(half_tokens, head_width)
-                    value = product(grads, r.weights[block_of(2, chunk)], 1, 0)
-                    r.total[:, half, :, place] += value.reshape(tensor_count, lines, part)
-                    for step in range(chips):
-                        other = 2 * lax.rem(chip + step, chips) + 1 - core
-                        r.hand_out[term, half, step, :, place] = r.total[
-                            other, half, :, place
-                        ].astype(low)
-                    hand_copy(term, half, chunk).start()
-
-                    @pl.when(chunk > 0)
-                    def _():
-                        hand_on(term, half, chunk - 1)
-
-                    if half:
-
-                        @pl.when(chunk == 0)
-                        def _():
-                            hand_on(term, half - 1, CHUNKS - 1)
-
-                    return carry
-
-                lax.fori_loop(0, CHUNKS, last, 0)
-            hand_on(term, HALVES - 1, CHUNKS - 1)
+                stage(half, 0, LAG, (half - 1, CHUNKS - LAG) if half else None)
+                stage(half, LAG, CHUNKS, (half, -LAG))
+            stage(None, CHUNKS - LAG, CHUNKS, (HALVES - 1, 0))
 
         def finish(term, half):
             for chunk in range(CHUNKS):
@@ -889,7 +898,7 @@
                 for step in range(1, chips):
                     value = value + r.far_in[term, half, step - 1, :, place].astype(full)
                 r.normed_grad[half, :, place] = value
-            scaled = r.scaled[0, half]
+            scaled = r.scaled[half]
             weighted = r.gain[...] * r.normed_grad[half]
             inner = jnp.sum(weighted * scaled, axis=1, keepdims=True)
             cotangent = inv_rms[half] * (weighted - scaled * (inner / width))
@@ -917,7 +926,7 @@
             for half in range(HALVES):
                 finish(term, half)
 
-        for item in range(2):
+        for item in range(3):
             gather_drain(item)
         for item in range(4):
             heads_drain(item)
@@ -961,7 +970,7 @@
             collective_id=0, has_side_effects=True, vmem_limit_bytes=58 << 20
         ),
     )(
-        fixed_point.reshape(HALVES, lines, width),
+        fixed_point,
         incoming,
         norm_gain.reshape(1, width),
         query_weight.reshape(CHUNKS, part, head_width),
@@ -972,8 +981,37 @@
         jnp.asarray(cosine),
         jnp.asarray(sine),
     )
-    adjoint = incoming.astype(full) + adjoint.reshape(rows, width)
-    return adjoint, gain_grad.reshape(width) * length ** (-0.5)
+
+    def close(incoming_hbm, part_hbm, gain_hbm, adjoint_ref, scaled_ref, base, other, gain, sems):
+        copies = [
+            pltpu.make_async_copy(incoming_hbm, base, sems.at[0]),
+            pltpu.make_async_copy(part_hbm, other, sems.at[1]),
+            pltpu.make_async_copy(gain_hbm, gain, sems.at[2]),
+        ]
+        for copy in copies:
+            copy.start()
+        for copy in copies:
+            copy.wait()
+        adjoint_ref[...] = base[...].astype(full) + other[...].reshape(rows, width)
+        scaled_ref[...] = gain[...] * length ** (-0.5)
+
+    adjoint, gain_grad = pl.pallas_call(
+        close,
+        out_shape=[
+            jax.ShapeDtypeStruct((rows, width), full),
+            jax.ShapeDtypeStruct((gain_rows, HEAD_DIM), full),
+        ],
+        in_specs=[anywhere] * 3,
+        out_specs=[pl.BlockSpec(memory_space=pltpu.VMEM)] * 2,
+        scratch_shapes=[
+            pltpu.VMEM((rows, width), low),
+            pltpu.VMEM((HALVES, lines, width), full),
+            pltpu.VMEM((gain_rows, HEAD_DIM), full),
+            dma((3,)),
+        ],
+        compiler_params=pltpu.CompilerParams(vmem_limit_bytes=60 << 20),
+    )(incoming, adjoint, gain_grad)
+    return adjoint, gain_grad.reshape(width)
 
 
 def solution(mesh):

time: 118 us -> 116 us (0.983)
  other arithmetic: 3.2 us -> 0 us
  Pallas kernels: 113 us -> 115 us
    pallas_call x0 -> x1, Pallas kernels: none -> 1.99 us  [fused_body(): pl.pallas_call(close, out_shape=[jax.ShapeDtypeStruct((rows, width), full...]
    add x1 -> x0, other arithmetic: 1.88 us -> none  [fused_body(): adjoint = incoming.astype(full) + adjoint.reshape(rows, width)]
    mul x1 -> x0, other arithmetic: 1.32 us -> none  [fused_body(): return (adjoint, gain_grad.reshape(width) * length ** (-0.5))]
where the time goes in v4:
time: 116 us
  Pallas kernels  115 us (99%)
    pallas_call x1, Pallas kernels, fused_body(): pl.pallas_call(kernel, out_shape=[jax.ShapeDtypeStruct((HALVES, lines, wi...  113 us

profile of v4, /device:TPU:0, one launch (start us, length us, event | category | flops | bytes accessed | tf_op | source)
XLA Modules:
  0.0 115.7 jit_solution(13708271558034019043)
XLA Ops:
  0.6 112.9 %shard_map.113 = (f32[2,16,4096]{2,1,0:T(8,128)}, f32[32,128]{1,0:T(8,128)}) custom-call(bf16[32,4096]{1,0:T(8,128)(2,1)} %refs_0_.1, bf16[32,4096]{1,0:T(8,128)(2,1)} %incoming_hbm.1, f32[1,4096]{1,0:T(1,128)} %bitcast.8, bf16[4,1024,1024]{2,1,0:T(8,128)(2,1)} %bitcast.5, bf16[4,1024,1024]{2,1,0:T(8,128)(2,1)} %bitcast.6, bf16[4,1024,1024]{2,1,0:T(8,128)(2,1)} %bitcast.7, ...), custom_call_target="tpu_custom_call" | custom-call | tf_op jit(solution)/shard_map/pallas_call | solution.py:960
  113.5 2.0 %shard_map.114 = (f32[32,4096]{1,0:T(8,128)}, f32[32,128]{1,0:T(8,128)}) custom-call(bf16[32,4096]{1,0:T(8,128)(2,1)} %incoming_hbm.1, f32[2,16,4096]{2,1,0:T(8,128)} %get-tuple-element.6.part_hbm, f32[32,128]{1,0:T(8,128)} %get-tuple-element.7.gain_hbm), custom_call_target="tpu_custom_call" | custom-call | tf_op jit(solution)/shard_map/pallas_call | solution.py:998

commit v5 on v4

--- a/solution.py
+++ b/solution.py
@@ -245,8 +245,8 @@
         "scaled": pltpu.VMEM((HALVES, lines, width), full),
         "pieces": pltpu.VMEM((3, tokens, width), low),
         "series": pltpu.VMEM((ITERS - 1, HALVES, tensor_count, lines, width), low),
-        "heads_out": pltpu.VMEM((4, seq_count, tokens, HEAD_DIM), low),
-        "heads_in": pltpu.VMEM((4, length, HEAD_DIM), low),
+        "heads_out": pltpu.VMEM((4, seq_count, tensor_count, HALVES, lines, HEAD_DIM), low),
+        "heads_in": pltpu.VMEM((4, groups, HALVES, lines, HEAD_DIM), low),
         "late_out": pltpu.VMEM(
             (ITERS - 1, HALVES, seq_count, tensor_count, lines, HEAD_DIM), low
         ),
@@ -271,9 +271,9 @@
         "gain_far": pltpu.VMEM((seq_count, gain_rows, HEAD_DIM), full),
         "load_sem": dma((6,)),
         "weight_sem": dma((CHUNKS + 1,)),
-        "gather_send": dma((3,)),
-        "gather_far": dma((3, CHUNKS * (chips - 1))),
-        "gather_near": dma((3, CHUNKS)),
+        "gather_send": dma((2 + HALVES,)),
+        "gather_far": dma((2 + HALVES, CHUNKS * (chips - 1))),
+        "gather_near": dma((2 + HALVES, CHUNKS)),
         "series_send": dma(((ITERS - 1) * HALVES,)),
         "series_far": dma(((ITERS - 1) * HALVES, CHUNKS * (chips - 1))),
         "series_near": dma(((ITERS - 1) * HALVES, CHUNKS)),
@@ -335,8 +335,8 @@
             load(4, cosine_hbm, r.cosine),
             load(5, sine_hbm, r.sine),
         ]
-        for index in (0, 1, 2, 3):
-            loads[index].start()
+        for copy in loads:
+            copy.start()
 
         def block_of(item, chunk):
             return item * CHUNKS + chunk
@@ -379,6 +379,11 @@
             place = window(chunk, part)
             if isinstance(item, tuple):
                 term, half = item
+                if term == 0:
+                    index = 0 if half == 0 else 2 + half
+                    start = pl.multiple_of(origin * rows + half * lines, lines)
+                    block = r.pieces.at[0, pl.ds(start, lines), place]
+                    return block, r.gather_send.at[index], r.gather_far, r.gather_near, index
                 index = (term - 1) * HALVES + half
                 block = r.series.at[term - 1, half, origin, :, place]
                 return block, r.series_send.at[index], r.series_far, r.series_near, index
@@ -414,7 +419,9 @@
         def gather_ready(item, chunk):
             place = window(chunk, part)
             block, send, far, near, index = gather_parts(item, chunk, 0)
-            if isinstance(item, tuple):
+            if isinstance(item, tuple) and item[0] == 0:
+                block = r.pieces.at[0, pl.ds(0, chips * lines), place]
+            elif isinstance(item, tuple):
                 block = r.series.at[item[0] - 1, item[1], pl.ds(0, chips), :, place]
             else:
                 block = r.pieces.at[item, pl.ds(0, chips * rows), place]
@@ -422,7 +429,9 @@
 
         def gather_drain(item):
             block, send, far, near, index = gather_parts(item, 0, 0)
-            if isinstance(item, tuple):
+            if isinstance(item, tuple) and item[0] == 0:
+                block = r.pieces.at[0, pl.ds(0, (2 * chips - 1) * lines), :]
+            elif isinstance(item, tuple):
                 block = r.series.at[item[0] - 1, item[1], pl.ds(0, 2 * chips - 1)]
             else:
                 block = r.pieces.at[item, pl.ds(0, (2 * chips - 1) * rows), :]
@@ -451,32 +460,43 @@
         def columns_of(slot):
             return slice(slot * head_width, (slot + 1) * head_width)
 
-        def heads_copy(item, mask):
+        def heads_copy(item, mask, half=None):
+            source = r.heads_out.at[item, mask]
+            target = r.heads_in.at[item, window(me_seq, tensor_count)]
+            if half is not None:
+                source, target = source.at[:, half], target.at[:, half]
             return remote(
-                r.heads_out.at[item, mask],
-                r.heads_in.at[item, own_tokens, :],
+                source,
+                target,
                 r.heads_send.at[item],
                 r.heads_recv.at[item],
                 "seq",
                 flipped(me_seq, mask, bits),
             )
 
-        def heads_start(item, turn):
+        def heads_start(item, turn, half=None):
+            part_rows = slice(None) if half is None else slice(half, half + 1)
+            count = tokens if half is None else half_tokens
+
+            def table(values):
+                values = values.reshape(tensor_count, HALVES, lines, HEAD_DIM)
+                return values[:, part_rows].reshape(count, HEAD_DIM)
+
             for mask in order + [0]:
                 peer = flipped(me_seq, mask, bits)
                 columns = window(item * seq_count + peer, HEAD_DIM)
-                values = r.total[:, :, :, columns].reshape(tokens, HEAD_DIM)
+                values = r.total[:, part_rows, :, columns].reshape(count, HEAD_DIM)
                 if turn:
-                    values = (
-                        values * r.cosine[own_tokens, :]
-                        + pltpu.roll(values, HEAD_DIM // 2, 1) * r.sine[own_tokens, :]
-                    )
+                    values = values * table(r.cosine[own_tokens, :]) + pltpu.roll(
+                        values, HEAD_DIM // 2, 1
+                    ) * table(r.sine[own_tokens, :])
+                values = values.astype(low).reshape(tensor_count, -1, lines, HEAD_DIM)
                 if mask:
-                    r.heads_out[item, mask] = values.astype(low)
+                    r.heads_out[item, mask, :, part_rows] = values
                 else:
-                    r.heads_in[item, own_tokens, :] = values.astype(low)
+                    r.heads_in[item, window(me_seq, tensor_count), part_rows] = values
             for mask in order:
-                heads_copy(item, mask).start()
+                heads_copy(item, mask, half).start()
 
         def late_copy(term, half, mask):
             index = (term - 1) * HALVES + half
@@ -507,7 +527,7 @@
             return remote(block, block, send, recv, "seq", flipped(me_seq, 1, bits))
 
         def heads_ready(item):
-            block = r.heads_in.at[item, pl.ds(0, (seq_count - 1) * tokens), :]
+            block = r.heads_in.at[item, pl.ds(0, (seq_count - 1) * tensor_count)]
             send, recv = r.heads_send.at[item], r.heads_recv.at[item]
             remote(block, block, send, recv, "seq", flipped(me_seq, 1, bits)).wait_recv()
 
@@ -630,8 +650,6 @@
                 weight_load(item, chunk).start()
         for chunk in range(CHUNKS):
             weight_load(3, chunk).start()
-        for copy in loads[4:]:
-            copy.start()
 
         point = r.pieces[2, own_rows, :].astype(full).reshape(HALVES, lines, width)
         inv_rms = lax.rsqrt(jnp.mean(point * point, axis=-1, keepdims=True) + EPS)
@@ -639,7 +657,8 @@
         normed = r.gain[...].reshape(1, 1, width) * r.scaled[...]
         r.pieces[0, own_rows, :] = normed.astype(low).reshape(rows, width)
         pl.semaphore_wait(barrier, tensor_count - 1 + seq_count - 1)
-        gather_start(0)
+        for half in range(HALVES):
+            gather_start((0, half))
 
         loads[3].wait()
         spread = (
@@ -660,25 +679,44 @@
         r.total[...] = jnp.zeros(r.total.shape, full)
         spread_rows = (tensor_count, HALVES, lines, head_width)
 
-        def project_one(item, chunk):
+        def project_one(item, half, chunk):
             place = window(chunk, part)
+            starts = [owner * rows + half * lines for owner in range(tensor_count)]
+            piece = jnp.concatenate(
+                [r.pieces[0, start : start + lines, place] for start in starts], axis=0
+            )
             weight = r.weights[1 + block_of(2 - item, chunk)]
-            value = product(r.pieces[0, :, place], weight, 1, 0)
-            r.total[:, :, :, columns_of(item)] += value.reshape(spread_rows)
-
-        def project(chunk):
+            value = product(piece, weight, 1, 0)
+            value = value.reshape(tensor_count, lines, head_width)
+            r.total[:, half, :, columns_of(item)] += value
+
+        def project(item, half):
+            def body(chunk, carry):
+                project_one(item, half, chunk)
+                return carry
+
+            lax.fori_loop(0, CHUNKS, body, 0)
+            heads_start(item, item < 2, half)
+
+        def project_first(chunk):
             weight_ready(chunk, 3)
-            for item in range(3):
-                project_one(item, chunk)
-
-        gather_each(0, project, lambda: gather_start(1), CHUNKS - 1)
+            project_one(0, 0, chunk)
+
+        gather_each((0, 0), project_first)
         for copy in loads[4:]:
             copy.wait()
-        gather_ready(0, CHUNKS - 1)
-        weight_ready(CHUNKS - 1, 3)
-        for item in range(3):
-            project_one(item, CHUNKS - 1)
-            heads_start(item, item < 2)
+        heads_start(0, True, 0)
+        project(1, 0)
+        for half in range(1, HALVES):
+            for chunk in range(CHUNKS):
+                gather_relay((0, half), chunk)
+        gather_start(1)
+        project(2, 0)
+        for half in range(1, HALVES):
+            for chunk in range(CHUNKS):
+                gather_ready((0, half), chunk)
+            for item in range(3):
+                project(item, half)
         weight_ready(CHUNKS, CHUNKS)
 
         def pull_first(chunk):
@@ -699,24 +737,25 @@
 
             return use
         gather_start(2)
-        turn_weights(0, 3)
-
-        for chunk in range(CHUNKS):
-            gather_relay(2, chunk)
-        for chunk in range(CHUNKS):
-            gather_ready(2, chunk)
+        turn_weights(0, 1)
 
         group = 2 if seq_count % 2 == 0 else 1
         heads_ready(0)
         heads_ready(1)
         sub = tokens // BLK
 
+        def head_rows(item, first, count):
+            block = r.heads_in[item, pl.ds(first * tensor_count, count * tensor_count)]
+            return block.reshape(count * tokens, HEAD_DIM)
+
         def forward(base):
             span = (base + group) * tokens
 
             def body(step, carry):
                 place = window(base + step, tokens)
-                scores = product(r.heads_in[0, place, :], r.heads_in[1, :span, :], 1, 1) * score_scale
+                scores = product(
+                    head_rows(0, base + step, 1), head_rows(1, 0, base + group), 1, 1
+                ) * score_scale
                 query_at = (base + step) * tokens + lax.broadcasted_iota(jnp.int32, (tokens, span), 0)
                 key_at = lax.broadcasted_iota(jnp.int32, (tokens, span), 1)
                 same = (query_at // BLK == key_at // BLK) & (key_at <= query_at)
@@ -748,7 +787,7 @@
 
         def grad_rows(term, first, count):
             if term == 0:
-                return r.heads_in[3, pl.ds(first * tokens, count * tokens), :]
+                return head_rows(3, first, count)
             block = r.late_in[term - 1, pl.ds(first * tensor_count, count * tensor_count)]
             return block.reshape(count * tokens, HEAD_DIM)
 
@@ -774,15 +813,15 @@
                     place = window(at_block, tokens)
                     probs = r.probs[place, :span]
                     grad_low = grad_rows(term, at_block, 1)
-                    grad_probs = product(grad_low, r.heads_in[2, :span, :], 1, 1)
+                    grad_probs = product(grad_low, head_rows(2, 0, base + group), 1, 1)
                     wide = probs.astype(full)
                     delta = jnp.sum(wide * grad_probs, axis=1, keepdims=True)
                     grad_scores = (wide * (grad_probs - delta)).astype(low)
-                    grad_query = product(grad_scores, r.heads_in[1, :span, :], 1, 0) * score_scale
+                    grad_query = product(grad_scores, head_rows(1, 0, base + group), 1, 0) * score_scale
                     r.query_out[term, window(at_block, tensor_count)] = turned_back(
                         grad_query, place
                     ).reshape(tensor_count, HALVES, lines, HEAD_DIM)
-                    r.key_acc[:span, :] += product(grad_scores, r.heads_in[0, place, :], 0, 0)
+                    r.key_acc[:span, :] += product(grad_scores, head_rows(0, at_block, 1), 0, 0)
                     return carry
 
                 lax.fori_loop(0, group, body, 0)
@@ -826,6 +865,10 @@
                 axis=0,
             )
         def invert():
+            for chunk in range(CHUNKS):
+                gather_relay(2, chunk)
+            for chunk in range(CHUNKS):
+                gather_ready(2, chunk)
             for owner in range(tensor_count):
                 place = slice(owner * rows, (owner + 1) * rows)
                 point = r.pieces[2, place, :].astype(full)
@@ -834,10 +877,11 @@
 
         def push(term):
             if term == 0:
-                invert()
+                turn_weights(1, 2)
             for item in (1, 0):
                 if term == 0 and item == 0:
-                    turn_weights(3, 4)
+                    turn_weights(2, 3)
+                    invert()
                 grads_ready(2 * term + item)
 
                 def body(chunk, carry):
@@ -925,8 +969,10 @@
             push(term)
             for half in range(HALVES):
                 finish(term, half)
-
-        for item in range(3):
+                if term + half == 0:
+                    turn_weights(3, 4)
+
+        for item in [(0, half) for half in range(HALVES)] + [1, 2]:
             gather_drain(item)
         for item in range(4):
             heads_drain(item)

time: 116 us -> 113 us (0.974)
  Pallas kernels: 115 us -> 112 us
    pallas_call x1, Pallas kernels: 113 us -> 110 us  [fused_body(): pl.pallas_call(kernel, out_shape=[jax.ShapeDtypeStruct((HALVES, lines, wi...]
where the time goes in v5:
time: 113 us
  Pallas kernels  112 us (99%)
    pallas_call x1, Pallas kernels, fused_body(): pl.pallas_call(kernel, out_shape=[jax.ShapeDtypeStruct((HALVES, lines, wi...  110 us

profile of v5, /device:TPU:0, one launch (start us, length us, event | category | flops | bytes accessed | tf_op | source)
XLA Modules:
  0.0 112.7 jit_solution(12867547764723336836)
XLA Ops:
  0.6 110.0 %shard_map.113 = (f32[2,16,4096]{2,1,0:T(8,128)}, f32[32,128]{1,0:T(8,128)}) custom-call(bf16[32,4096]{1,0:T(8,128)(2,1)} %refs_0_.1, bf16[32,4096]{1,0:T(8,128)(2,1)} %incoming_hbm.1, f32[1,4096]{1,0:T(1,128)} %bitcast.8, bf16[4,1024,1024]{2,1,0:T(8,128)(2,1)} %bitcast.5, bf16[4,1024,1024]{2,1,0:T(8,128)(2,1)} %bitcast.6, bf16[4,1024,1024]{2,1,0:T(8,128)(2,1)} %bitcast.7, ...), custom_call_target="tpu_custom_call" | custom-call | tf_op jit(solution)/shard_map/pallas_call | solution.py:1006
  110.6 2.0 %shard_map.114 = (f32[32,4096]{1,0:T(8,128)}, f32[32,128]{1,0:T(8,128)}) custom-call(bf16[32,4096]{1,0:T(8,128)(2,1)} %incoming_hbm.1, f32[2,16,4096]{2,1,0:T(8,128)} %get-tuple-element.6.part_hbm, f32[32,128]{1,0:T(8,128)} %get-tuple-element.7.gain_hbm), custom_call_target="tpu_custom_call" | custom-call | tf_op jit(solution)/shard_map/pallas_call | solution.py:1044
